TPU v7x, 32 devices: a whole 2x2x4 slice. The times are simulated.
32 devices in a mesh: mem: 4 (over z), reg: 8 (over y, x, core).
Axes of the slice: x: 2, y: 2, z: 4, core: 2. Of those that a mesh axis runs over, the one named last changes fastest.
Arguments:
- member_values: float32 [40, 32768], P('mem', 'reg'), may hold values from -6 to 6
- obs_value: float32 [32768], P('reg'), may hold values from -6 to 6
- obs_weight: float32 [32768], P('reg'), may hold values from 0.25 to 4
- obs_cell: int32 [32768], P('reg'), may hold values from -1 to 15359, as said below
Outputs:
- deviation: float32 [40, 15360], P('mem', 'reg')
- departure: float32 [15360], P('reg')
- variance: float32 [15360], P('reg')
- error_variance: float32 [15360], P('reg')
- obs_total: int32 [15360], P('reg')
Inputs may be any that keep to these rules, and one draw needn't show every extreme that they name: `obs_cell`: cell c is owned by region c // 1920. The 4096 slots of one region are 8 blocks of 512 slots, block r holding only cells owned by region r, live slots first and -1 in the empty ones. Every block has at least 128 live slots; one owner's block is full in every region.
All inputs are finite; a program needn't handle non-finite values.
Results may differ from a plain program's by a relative error of at most 0.0003.
Values sent between devices are 32-bit elements; how exact they have to be, the bound alone decides.
No kernel may reach another device: no remote copies, remote signals or barrier semaphores. Data moves between devices by JAX's collectives and lax.ppermute only.
A program may use at most 64 MiB of HBM per device.

v0:
```python
import jax
import jax.numpy as jnp
from jax import lax
from jax.sharding import PartitionSpec as P

CELL_DEV = 1920


def shards(member_values, obs_value, obs_weight, obs_cell):
    regions = lax.axis_size("reg")
    groups = lax.axis_size("mem")
    obs_dev = obs_cell.shape[0]
    capacity = obs_dev // regions
    live = obs_cell >= 0
    weight = jnp.where(live, obs_weight, jnp.float32(0.0))
    local_cell = jnp.where(live, obs_cell % CELL_DEV, 0).astype(jnp.float32)
    weighted_members = member_values * weight[None, :]
    meta_rows = jnp.stack([weight * obs_value, weight, local_cell])
    member_buffer = weighted_members.reshape(weighted_members.shape[0], regions, capacity)
    meta_buffer = meta_rows.reshape(3, regions, capacity)
    payload = jnp.concatenate([member_buffer, meta_buffer], 0)
    received = lax.all_to_all(payload, "reg", split_axis=1, concat_axis=1, tiled=True)
    received = received.reshape(received.shape[0], -1)
    members_in = received[:-3]
    meta_in = received[-3:]
    cell_in = meta_in[2].astype(jnp.int32)
    filled_flag = (meta_in[1] > 0).astype(jnp.float32)
    columns = jnp.concatenate([members_in, meta_in[:2], filled_flag[None, :]], 0)
    total_rows = columns.shape[1]
    block_rows = 1024
    column_blocks = columns.reshape(
        columns.shape[0], total_rows // block_rows, block_rows
    ).transpose(1, 0, 2)
    cell_blocks = cell_in.reshape(total_rows // block_rows, block_rows)
    cell_range = jnp.arange(CELL_DEV, dtype=jnp.int32)

    def add_block(carry, inputs):
        block_columns, block_cells = inputs
        one_hot = (block_cells[:, None] == cell_range[None, :]).astype(jnp.float32)
        return (
            carry
            + jnp.dot(
                block_columns,
                one_hot,
                precision=lax.Precision.HIGHEST,
                preferred_element_type=jnp.float32,
            ),
            None,
        )

    start_sums = jnp.zeros((columns.shape[0], CELL_DEV), jnp.float32)
    cell_sums, _ = lax.scan(add_block, start_sums, (column_blocks, cell_blocks))
    counted = cell_sums[-1]
    filled = counted > 0
    weight_total = jnp.where(filled, cell_sums[-2], jnp.float32(1.0))
    superob = cell_sums[:-3] / weight_total[None, :]
    observed_mean = cell_sums[-3] / weight_total
    ensemble = member_values.shape[0] * groups
    moment_one, moment_two = lax.psum((jnp.sum(superob, 0), jnp.sum(superob * superob, 0)), "mem")
    ens_mean = moment_one / ensemble
    deviation = superob - ens_mean[None, :]
    variance = (moment_two - moment_one * ens_mean) / (ensemble - 1)
    departure = observed_mean - ens_mean
    error_variance = jnp.where(filled, 1.0 / weight_total, jnp.float32(0.0))
    return (deviation, departure, variance, error_variance, counted.astype(jnp.int32))


def solution(mesh):
    return jax.shard_map(
        shards,
        mesh=mesh,
        in_specs=(P("mem", "reg"), P("reg"), P("reg"), P("reg")),
        out_specs=(P("mem", "reg"), P("reg"), P("reg"), P("reg"), P("reg")),
        check_vma=False,
    )
```

profile of v0, /device:TPU:0, one launch (start us, length us, event | category | flops | bytes accessed | tf_op | source)
XLA Modules:
  0.0 48.5 jit_solution(72465091545235863)
XLA Ops:
  0.6 0.7 %fusion.6 = f32[4096]{0:T(1024)S(1)} fusion(s32[4096]{0:T(1024)} %param.9), kind=kLoop, calls=%fused_computation.17 | loop fusion | flops 36864 | bytes 32768 | tf_op jit(solution)/shard_map/convert_element_type | solution.py:16
  1.4 0.8 %fusion.11 = (f32[4096]{0:T(1024)S(1)}, f32[4096]{0:T(1024)S(1)}) fusion(f32[4096]{0:T(1024)} %param.7, f32[4096]{0:T(1024)} %param.8, s32[4096]{0:T(1024)} %param.9), kind=kLoop, calls=%fused_computation.34 | loop fusion | flops 12288 | bytes 81920 | tf_op jit(solution)/shard_map/mul | solution.py:18
  2.1 1.0 %broadcast_multiply_fusion = f32[10,4096]{1,0:T(8,128)S(1)} fusion(f32[10,4096]{1,0:T(8,128)} %param.6, f32[4096]{0:T(1024)S(1)} %get-tuple-element.78), kind=kLoop, calls=%fused_computation.10 | loop fusion | flops 40960 | bytes 344064 | tf_op jit(solution)/shard_map/mul | solution.py:17
  3.1 0.2 copy.18
  3.3 0.8 %copy.13 = f32[13,8,512]{2,0,1:T(8,128)} copy(f32[13,8,512]{2,1,0:T(8,128)S(1)} %pad_maximum_fusion) | data formatting | bytes 425984 | tf_op jit(solution)/shard_map/concatenate | solution.py:21
  4.2 5.2 %all-to-all-start = ((f32[13,8,512]{2,0,1:T(8,128)}), f32[13,8,512]{2,0,1:T(8,128)S(1)}, u32[]{:S(2)}, u32[]{:S(2)}) async-start(f32[13,8,512]{2,0,1:T(8,128)} %copy.13), calls=%async_computation | async-start | bytes 524288 | tf_op jit(solution)/shard_map/all_to_all | solution.py:22
  9.4 6.9 %all-to-all-done = f32[13,8,512]{2,0,1:T(8,128)S(1)} async-done(((f32[13,8,512]{2,0,1:T(8,128)}), f32[13,8,512]{2,0,1:T(8,128)S(1)}, u32[]{:S(2)}, u32[]{:S(2)}) %all-to-all-start) | async-done | bytes 213024 | tf_op jit(solution)/shard_map/all_to_all | solution.py:22
  16.3 0.1 copy.14
  16.4 0.1 concatenate.14
  16.5 0.1 fusion.7
  16.6 0.1 fusion.8
  16.7 0.1 maximum_bitcast_fusion
  16.8 10.7 %while.11 = (s32[]{:T(128)}, f32[13,1920]{1,0:T(8,128)S(1)}, f32[4,13,1024]{2,0,1:T(4,128)S(1)}, s32[4,1024]{1,0:T(4,128)S(1)}, s32[]{:T(128)}, /*index=5*/s32[]{:T(128)}) while((s32[]{:T(128)}, f32[13,1920]{1,0:T(8,128)S(1)}, f32[4,13,1024]{2,0,1:T(4,128)S(1)}, s32[4,1024]{1,0:T(4,128)S(1)}, s32[]{:T(128)}, ...), condition=%wide.region_1.2_spmd.clone, body=%wide.region_0.1_spmd.clone.sunk | while | flops 308724480 | bytes 371799 | solution.py:52
  16.8 0.1 constant_dynamic-slice_fusion.5
  16.9 2.6 %fusion.13 = f32[13,1920]{1,0:T(8,128)S(1)} fusion(s32[1024]{0:T(1024)S(1)} %bitcast.17, f32[13,1920]{1,0:T(8,128)S(1)} %get-tuple-element.115, f32[1,13,1024]{2,0,1:T(1,128)S(1)} %constant_dynamic-slice_fusion.5, pred[]{:T(512)S(6)} %compare.3), kind=kOutput, calls=%fused_computation.4.clone.1 | convolution fusion | flops 308724480 | bytes 257025 | tf_op jit(solution)/shard_map/while/body/eval_jaxpr/dot_general | solution.py:42
  19.4 0.1 constant_dynamic-slice_fusion.5
  19.5 2.6 %fusion.13 = f32[13,1920]{1,0:T(8,128)S(1)} fusion(s32[1024]{0:T(1024)S(1)} %bitcast.17, f32[13,1920]{1,0:T(8,128)S(1)} %get-tuple-element.115, f32[1,13,1024]{2,0,1:T(1,128)S(1)} %constant_dynamic-slice_fusion.5, pred[]{:T(512)S(6)} %compare.3), kind=kOutput, calls=%fused_computation.4.clone.1 | convolution fusion | flops 308724480 | bytes 257025 | tf_op jit(solution)/shard_map/while/body/eval_jaxpr/dot_general | solution.py:42
  22.1 0.1 constant_dynamic-slice_fusion.5
  22.2 2.6 %fusion.13 = f32[13,1920]{1,0:T(8,128)S(1)} fusion(s32[1024]{0:T(1024)S(1)} %bitcast.17, f32[13,1920]{1,0:T(8,128)S(1)} %get-tuple-element.115, f32[1,13,1024]{2,0,1:T(1,128)S(1)} %constant_dynamic-slice_fusion.5, pred[]{:T(512)S(6)} %compare.3), kind=kOutput, calls=%fused_computation.4.clone.1 | convolution fusion | flops 308724480 | bytes 257025 | tf_op jit(solution)/shard_map/while/body/eval_jaxpr/dot_general | solution.py:42
  24.8 0.1 constant_dynamic-slice_fusion.5
  24.9 2.6 %fusion.13 = f32[13,1920]{1,0:T(8,128)S(1)} fusion(s32[1024]{0:T(1024)S(1)} %bitcast.17, f32[13,1920]{1,0:T(8,128)S(1)} %get-tuple-element.115, f32[1,13,1024]{2,0,1:T(1,128)S(1)} %constant_dynamic-slice_fusion.5, pred[]{:T(512)S(6)} %compare.3), kind=kOutput, calls=%fused_computation.4.clone.1 | convolution fusion | flops 308724480 | bytes 257025 | tf_op jit(solution)/shard_map/while/body/eval_jaxpr/dot_general | solution.py:42
  27.5 0.1 slice_reduce_fusion.1
  27.6 0.6 %convert_reduce_fusion = s32[1920]{0:T(1024)} fusion(f32[13,1920]{1,0:T(8,128)S(1)} %get-tuple-element.32), kind=kLoop, calls=%fused_computation.29 | loop fusion | flops 1920 | bytes 15360 | tf_op jit(solution)/shard_map/convert_element_type | solution.py:65
  28.2 0.1 multiply_reduce_fusion
  28.3 19.0 %all-reduce = (f32[1920]{0:T(1024)S(1)}, f32[1920]{0:T(1024)S(1)}) all-reduce(f32[1920]{0:T(1024)S(1)} %get-tuple-element.63, f32[1920]{0:T(1024)S(1)} %get-tuple-element.62), channel_id=1, replica_groups=mesh['mem'=4,'reg'=8] {'mem'}, use_global_device_ids=true, to_apply=%region_3.4 | all-reduce | flops 3840 | bytes 30720 | tf_op jit(solution)/shard_map/psum | solution.py:59
  47.3 0.6 %divide_select_fusion = (f32[1920]{0:T(1024)}, f32[1920]{0:T(1024)}, f32[1920]{0:T(1024)}, f32[1920]{0:T(1024)S(1)}) fusion(pred[1920]{0:T(1024)(128)(4,1)S(1)} %compare_reduce_fusion, f32[1920]{0:T(1024)S(1)} %get-tuple-element.64, f32[1920]{0:T(1024)S(1)} %get-tuple-element.75, f32[1920]{0:T(1024)S(1)} %get-tuple-element.65, f32[1920]{0:T(1024)S(1)} %get-tuple-element.76), kind=kLoop, calls=%fused_computation.23 | loop fusion | flops 17280 | bytes 63360 | tf_op jit(solution)/shard_map/jit(_where)/select_n | solution.py:64
  47.9 0.7 %broadcast_subtract_fusion = f32[10,1920]{1,0:T(8,128)} fusion(f32[1920]{0:T(1024)S(1)} %get-tuple-element.82, f32[1920]{0:T(1024)S(1)} %get-tuple-element.66, f32[13,1920]{1,0:T(8,128)S(1)} %get-tuple-element.32), kind=kLoop, calls=%fused_computation.14 | loop fusion | flops 38400 | bytes 168960 | tf_op jit(solution)/shard_map/sub | solution.py:61
  (16 shorter events, 0.2 us)
Async XLA Ops:
  4.2 12.1 %all-to-all-start = ((f32[13,8,512]{2,0,1:T(8,128)}), f32[13,8,512]{2,0,1:T(8,128)S(1)}, u32[]{:S(2)}, u32[]{:S(2)}) async-start(f32[13,8,512]{2,0,1:T(8,128)} %copy.13), calls=%async_computation | async-start | bytes 524288 | tf_op jit(solution)/shard_map/all_to_all | solution.py:22
where the time goes:
time: 49 us; the launch traced here: 48.5 us
  blocking collectives  19 us (39%)
  matrix products  10.3 us (21%)
  waiting for transfers between devices  6.9 us (14%)
  starting transfers between devices  5.2 us (11%)
  other arithmetic  4.73 us (10%)
  local copies, waits for them, and re-layouts  1.52 us (3%)
  between operations  0.77 us (2%)
    psum x1, blocking collectives, shards(): lax.psum((jnp.sum(superob, 0), jnp.sum(superob * superob, 0)), 'mem')  19 us
    dot_general x4, matrix products, add_block(): jnp.dot(block_columns, one_hot, precision=lax.Precision.HIGHEST, preferre...  10.3 us
    all_to_all x1, waiting for transfers between devices, shards(): lax.all_to_all(payload, 'reg', split_axis=1, concat_axis=1, tiled=True)  6.9 us
    all_to_all x1, starting transfers between devices, shards(): lax.all_to_all(payload, 'reg', split_axis=1, concat_axis=1, tiled=True)  5.2 us
  transfers between devices with their start and end apart: 1, of which 1 were waited for; matrix products, arithmetic and copies ran while one was open for 0% of the time, Pallas kernels for 0%

commit v1 on v0

v1 whole, which is shorter than its diff:
```python
import functools
import jax
import jax.numpy as jnp
from jax import lax
from jax.experimental import pallas as pl
from jax.experimental.pallas import tpu as pltpu
from jax.sharding import PartitionSpec as P

CELL_DEV = 1920
LANES = 128
WIDE = 256


def round_up(size, unit):
    return -(-size // unit) * unit


def block_rows(members):
    rows = round_up(members + 2, 4)
    return rows, rows // 8 * 8


def pack_kernel(members, regions, chunks, value_ref, obs_ref, weight_ref, cell_ref, same_ref, other_ref):
    me = lax.axis_index("reg")
    rows, whole = block_rows(members)
    rest = rows - whole
    for step in range(regions):
        owner = me ^ step
        out_ref = other_ref if step % 2 else same_ref
        for j in range(chunks):
            line = owner * chunks + j
            values = value_ref[:, pl.ds(pl.multiple_of(line * LANES, LANES), LANES)]
            cell = cell_ref[pl.ds(line, 1), :]
            live = cell >= 0
            weight = jnp.where(live, weight_ref[pl.ds(line, 1), :], 0.0)
            local = jnp.where(live, cell - owner * CELL_DEV, -1).astype(jnp.float32)
            innovation = (values - obs_ref[pl.ds(line, 1), :]) * weight
            tail = whole * chunks + j * rest
            out_ref[step // 2, pl.ds(j * whole, whole), :] = innovation[:whole]
            out_ref[step // 2, pl.ds(tail, members - whole), :] = innovation[whole:]
            out_ref[step // 2, pl.ds(tail + members - whole, 1), :] = weight
            out_ref[step // 2, pl.ds(tail + members - whole + 1, 1), :] = local


def bin_kernel(members, chunks, groups, in_refs, dev_ref, moment_ref, error_ref, count_ref, acc_ref):
    rows, whole = block_rows(members)
    rest = rows - whole
    pad = round_up(rows, 16)
    low_iota = lax.broadcasted_iota(jnp.int32, (WIDE, LANES), 0)
    row_iota = lax.broadcasted_iota(jnp.int32, (pad, LANES), 0)
    blocks = [(ref, b) for ref, picks in in_refs for b in picks]
    for n, (ref, b) in enumerate(blocks):
        parts, lows, highs = [], [], []
        for j in range(chunks):
            tail = whole * chunks + j * rest
            values = jnp.concatenate(
                [
                    ref[b, pl.ds(j * whole, whole), :],
                    ref[b, pl.ds(tail, rest), :],
                    jnp.zeros((pad - rows, LANES), jnp.float32),
                ],
                0,
            )
            cell = ref[b, pl.ds(tail + members - whole + 1, 1), :].astype(jnp.int32)
            live = (cell >= 0).astype(jnp.float32)
            values = jnp.where(row_iota == members + 1, live, values)
            top = values.astype(jnp.bfloat16)
            left_over = values - top.astype(jnp.float32)
            middle = left_over.astype(jnp.bfloat16)
            bottom = (left_over - middle.astype(jnp.float32)).astype(jnp.bfloat16)
            parts.append(jnp.concatenate([top, middle, bottom], 0))
            high = lax.shift_right_arithmetic(cell, 8)
            highs.append(jnp.broadcast_to(high, (3 * pad, LANES)))
            lows.append((low_iota == (cell & (WIDE - 1))).astype(jnp.float32).astype(jnp.bfloat16))
        part = jnp.concatenate(parts, 1)
        high = jnp.concatenate(highs, 1)
        low = jnp.concatenate(lows, 1)
        left = jnp.concatenate(
            [jnp.where(high == g, part, jnp.zeros_like(part)) for g in range(groups)], 0
        )
        product = lax.dot_general(
            left, low, (((1,), (1,)), ((), ())), preferred_element_type=jnp.float32
        )
        if n == 0:
            acc_ref[...] = product
        else:
            acc_ref[...] += product
    for g in range(groups):
        start, width = g * WIDE, min(WIDE, CELL_DEV - g * WIDE)
        base = g * 3 * pad
        sums = (
            acc_ref[pl.ds(base, pad), :width]
            + acc_ref[pl.ds(base + pad, pad), :width]
            + acc_ref[pl.ds(base + 2 * pad, pad), :width]
        )
        counted = sums[members + 1 : members + 2]
        filled = counted > 0
        total = jnp.where(filled, sums[members : members + 1], 1.0)
        deviation = sums[:members] / total
        moment = jnp.sum(deviation, 0, keepdims=True)
        centred = deviation - moment / members
        spread = jnp.sum(centred * centred, 0, keepdims=True)
        error = jnp.where(filled, 1.0 / total, 0.0)
        count = counted.astype(jnp.int32)
        dev_ref[:, start : start + width] = deviation
        for j in range(width // LANES):
            line, cut = start // LANES + j, slice(j * LANES, (j + 1) * LANES)
            moment_ref[0, line : line + 1, :] = moment[:, cut]
            moment_ref[1, line : line + 1, :] = spread[:, cut]
            error_ref[line : line + 1, :] = error[:, cut]
            count_ref[line : line + 1, :] = count[:, cut]


def near(array):
    return pltpu.with_memory_space_constraint(array, pltpu.VMEM)


def bin_call(members, chunks, arrays):
    groups = -(-CELL_DEV // WIDE)
    pad = round_up(block_rows(members)[0], 16)

    def body(*refs):
        pairs = list(zip(refs, [picks for _, picks in arrays]))
        bin_kernel(members, chunks, groups, pairs, *refs[len(arrays) :])

    lines = CELL_DEV // LANES
    return pl.pallas_call(
        body,
        out_shape=[
            pltpu.VMEM((members, CELL_DEV), jnp.float32),
            pltpu.VMEM((2, lines, LANES), jnp.float32),
            pltpu.VMEM((lines, LANES), jnp.float32),
            pltpu.VMEM((lines, LANES), jnp.int32),
        ],
        scratch_shapes=[pltpu.VMEM((groups * 3 * pad, WIDE), jnp.float32)],
    )(*[near(array) for array, _ in arrays])


def final_kernel(
    total, dev_ref, mine_ref, theirs_ref, error_in, count_in, out_ref, departure_ref, variance_ref, error_ref, count_ref
):
    half = total // 2
    moment = mine_ref[0] + theirs_ref[0]
    gap = mine_ref[0] - theirs_ref[0]
    spread = mine_ref[1] + theirs_ref[1] + gap * gap / (2 * half)
    mean = moment / total
    departure_ref[...] = -mean
    variance_ref[...] = spread / (total - 1)
    error_ref[...] = error_in[...]
    count_ref[...] = count_in[...]
    for j in range(CELL_DEV // LANES):
        cut = slice(j * LANES, (j + 1) * LANES)
        out_ref[:, cut] = dev_ref[:, cut] - mean[j : j + 1]


def merge(mine, theirs, each):
    gap = mine[0] - theirs[0]
    return jnp.stack([mine[0] + theirs[0], mine[1] + theirs[1] + gap * gap / (2 * each)])


def shards(member_values, obs_value, obs_weight, obs_cell):
    regions = lax.axis_size("reg")
    groups = lax.axis_size("mem")
    members, slots = member_values.shape
    chunks = slots // regions // LANES
    chips = regions // 2
    f32 = functools.partial(jax.ShapeDtypeStruct, dtype=jnp.float32)
    lines = (slots // LANES, LANES)
    same, other = pl.pallas_call(
        functools.partial(pack_kernel, members, regions, chunks),
        out_shape=[pltpu.VMEM((chips, chunks * block_rows(members)[0], LANES), jnp.float32)] * 2,
    )(member_values, obs_value.reshape(lines), obs_weight.reshape(lines), obs_cell.reshape(lines))
    partner = lax.ppermute(other, "reg", [(i, i ^ 1) for i in range(regions)])
    arrays = [(same, (0,)), (partner, (0,))]
    for k in range(chips - 1, 0, -1):
        sent = jnp.stack([same[k], partner[k]])
        arrays.append((lax.ppermute(sent, "reg", [(i, i ^ (2 * k)) for i in range(regions)]), (0, 1)))
    deviation, moments, error_variance, obs_total = bin_call(members, chunks, arrays)
    each, reach = members, 1
    while 2 * reach < groups:
        theirs = lax.ppermute(moments, "mem", [(i, i ^ reach) for i in range(groups)])
        moments = merge(moments, theirs, each)
        each, reach = 2 * each, 2 * reach
    theirs = lax.ppermute(moments, "mem", [(i, i ^ reach) for i in range(groups)])
    cells = (CELL_DEV // LANES, LANES)
    outs = pl.pallas_call(
        functools.partial(final_kernel, members * groups),
        out_shape=[f32((members, CELL_DEV)), f32(cells), f32(cells), f32(cells), jax.ShapeDtypeStruct(cells, jnp.int32)],
    )(*[near(a) for a in (deviation, moments, theirs, error_variance, obs_total)])
    return (outs[0], *[out.reshape(-1) for out in outs[1:]])


def solution(mesh):
    return jax.shard_map(
        shards,
        mesh=mesh,
        in_specs=(P("mem", "reg"), P("reg"), P("reg"), P("reg")),
        out_specs=(P("mem", "reg"), P("reg"), P("reg"), P("reg"), P("reg")),
        check_vma=False,
    )
```

time: 49 us -> 22.4 us (0.46)
  blocking collectives: 19 us -> 0 us
  matrix products: 10.3 us -> 0 us
  other arithmetic: 4.73 us -> 0.03 us
  starting transfers between devices: 5.2 us -> 9.5 us
  Pallas kernels: 0 us -> 3.1 us
  waiting for transfers between devices: 6.9 us -> 8.95 us
  local copies, waits for them, and re-layouts: 1.52 us -> 0.01 us
    psum x1 -> x0, blocking collectives: 19 us -> none  [shards(): lax.psum((jnp.sum(superob, 0), jnp.sum(superob * superob, 0)), 'mem')]
    dot_general x4 -> x0, matrix products: 10.3 us -> none  [add_block(): jnp.dot(block_columns, one_hot, precision=lax.Precision.HIGHEST, preferre...]
    ppermute x0 -> x6, starting transfers between devices: none -> 9.5 us  [the longest x3 4.5 us: shards(): lax.ppermute(sent, 'reg', [(i, i ^ 2 * k) for i in range(regions)])]
    ppermute x0 -> x6, waiting for transfers between devices: none -> 8.95 us  [the longest x2 4.07 us: shards(): lax.ppermute(moments, 'mem', [(i, i ^ reach) for i in range(groups)])]
    all_to_all x1 -> x0, waiting for transfers between devices: 6.9 us -> none  [shards(): lax.all_to_all(payload, 'reg', split_axis=1, concat_axis=1, tiled=True)]
    all_to_all x1 -> x0, starting transfers between devices: 5.2 us -> none  [shards(): lax.all_to_all(payload, 'reg', split_axis=1, concat_axis=1, tiled=True)]
    pallas_call x0 -> x3, Pallas kernels: none -> 3.1 us  [the longest x1 1.37 us: bin_call(): pl.pallas_call(body, out_shape=[pltpu.VMEM((members, CELL_DEV), jnp.float...]
    mul x2 -> x0, other arithmetic: 1.73 us -> none  [the longest x1 0.97 us: shards(): weighted_members = member_values * weight[None, :]]
  transfers between devices with their start and end apart: 1 -> 6, of which waited for: 1 -> 6; matrix products, arithmetic and copies ran while one was open for 0% -> 0% of each run, Pallas kernels for 0% -> 0%
where the time goes in v1:
time: 22.4 us; the launch traced here: 22.2 us
  starting transfers between devices  9.5 us (42%)
  waiting for transfers between devices  8.95 us (40%)
  Pallas kernels  3.1 us (14%)
  between operations  0.65 us (3%)
    ppermute x3, starting transfers between devices, shards(): lax.ppermute(sent, 'reg', [(i, i ^ 2 * k) for i in range(regions)])  4.5 us
    ppermute x2, starting transfers between devices, shards(): lax.ppermute(moments, 'mem', [(i, i ^ reach) for i in range(groups)])  4.44 us
    ppermute x2, waiting for transfers between devices, shards(): lax.ppermute(moments, 'mem', [(i, i ^ reach) for i in range(groups)])  4.07 us
    ppermute x3, waiting for transfers between devices, shards(): lax.ppermute(sent, 'reg', [(i, i ^ 2 * k) for i in range(regions)])  3.94 us
    pallas_call x1, Pallas kernels, bin_call(): pl.pallas_call(body, out_shape=[pltpu.VMEM((members, CELL_DEV), jnp.float...  1.37 us
    pallas_call x1, Pallas kernels, shards(): pl.pallas_call(functools.partial(pack_kernel, members, regions, chunks),...  1.05 us
    ppermute x1, waiting for transfers between devices, shards(): partner = lax.ppermute(other, 'reg', [(i, i ^ 1) for i in range(regions)])  0.94 us
    pallas_call x1, Pallas kernels, shards(): pl.pallas_call(functools.partial(final_kernel, members * groups), out_sha...  0.67 us
  transfers between devices with their start and end apart: 6, of which 6 were waited for; matrix products, arithmetic and copies ran while one was open for 0% of the time, Pallas kernels for 0%

profile of v1, /device:TPU:0, one launch (start us, length us, event | category | flops | bytes accessed | tf_op | source)
XLA Modules:
  0.0 22.2 jit_solution(17790780528421927277)
XLA Ops:
  0.6 1.1 %shard_map.83 = (f32[4,48,128]{2,1,0:T(8,128)S(1)}, f32[4,48,128]{2,1,0:T(8,128)S(1)}) custom-call(f32[10,4096]{1,0:T(8,128)} %value_ref.1, f32[32,128]{1,0:T(8,128)} %bitcast.7, f32[32,128]{1,0:T(8,128)} %bitcast.8, s32[32,128]{1,0:T(8,128)} %bitcast.9), custom_call_target="tpu_custom_call" | custom-call | tf_op jit(solution)/shard_map/pallas_call | solution.py:169
  1.7 0.6 %collective-permute-start = (f32[4,48,128]{2,1,0:T(8,128)S(1)}, f32[4,48,128]{2,1,0:T(8,128)S(1)}, u32[]{:S(2)}, u32[]{:S(2)}) collective-permute-start(f32[4,48,128]{2,1,0:T(8,128)S(1)} %get-tuple-element.17), channel_id=1, source_target_pairs={{0,1},{1,0},{2,3},{3,2},{4,5},{5,4},{6,7},{7,6},{8,9},{9,8},{10,11... | collective-permute-start | bytes 294920 | tf_op jit(solution)/shard_map/ppermute | solution.py:173
  2.2 0.9 %collective-permute-done.refs_1_ = f32[4,48,128]{2,1,0:T(8,128)S(1)} collective-permute-done((f32[4,48,128]{2,1,0:T(8,128)S(1)}, f32[4,48,128]{2,1,0:T(8,128)S(1)}, u32[]{:S(2)}, u32[]{:S(2)}) %collective-permute-start) | collective-permute-done | bytes 98336 | tf_op jit(solution)/shard_map/ppermute | solution.py:173
  3.2 3.9 %collective-permute-start.1 = (f32[2,48,128]{2,1,0:T(8,128)S(1)}, f32[2,48,128]{2,1,0:T(8,128)S(1)}, u32[]{:S(2)}, u32[]{:S(2)}) collective-permute-start(f32[2,48,128]{2,1,0:T(8,128)S(1)} %pad_maximum_fusion), channel_id=1, source_target_pairs={{0,6},{1,7},{2,4},{3,5},{4,2},{5,3},{6,0},{7,1},{8,14},{9,15},{10,... | collective-permute-start | bytes 147464 | tf_op jit(solution)/shard_map/ppermute | solution.py:177
  7.1 0.5 %collective-permute-start.2 = (f32[2,48,128]{2,1,0:T(8,128)S(1)}, f32[2,48,128]{2,1,0:T(8,128)S(1)}, u32[]{:S(2)}, u32[]{:S(2)}) collective-permute-start(f32[2,48,128]{2,1,0:T(8,128)S(1)} %pad_maximum_fusion.1), channel_id=1, source_target_pairs={{0,4},{1,5},{2,6},{3,7},{4,0},{5,1},{6,2},{7,3},{8,12},{9,13},{10,... | collective-permute-start | bytes 147464 | tf_op jit(solution)/shard_map/ppermute | solution.py:177
  7.6 0.1 collective-permute-start.3
  7.7 1.4 %collective-permute-done.1.refs_2_ = f32[2,48,128]{2,1,0:T(8,128)S(1)} collective-permute-done((f32[2,48,128]{2,1,0:T(8,128)S(1)}, f32[2,48,128]{2,1,0:T(8,128)S(1)}, u32[]{:S(2)}, u32[]{:S(2)}) %collective-permute-start.1) | collective-permute-done | bytes 49184 | tf_op jit(solution)/shard_map/ppermute | solution.py:177
  9.1 2.0 %collective-permute-done.2.refs_3_ = f32[2,48,128]{2,1,0:T(8,128)S(1)} collective-permute-done((f32[2,48,128]{2,1,0:T(8,128)S(1)}, f32[2,48,128]{2,1,0:T(8,128)S(1)}, u32[]{:S(2)}, u32[]{:S(2)}) %collective-permute-start.2) | collective-permute-done | bytes 49184 | tf_op jit(solution)/shard_map/ppermute | solution.py:177
  11.2 0.5 %collective-permute-done.3.refs_4_ = f32[2,48,128]{2,1,0:T(8,128)S(1)} collective-permute-done((f32[2,48,128]{2,1,0:T(8,128)S(1)}, f32[2,48,128]{2,1,0:T(8,128)S(1)}, u32[]{:S(2)}, u32[]{:S(2)}) %collective-permute-start.3) | collective-permute-done | bytes 49184 | tf_op jit(solution)/shard_map/ppermute | solution.py:177
  11.7 1.4 %shard_map.84 = (f32[10,1920]{1,0:T(8,128)S(1)}, f32[2,15,128]{2,1,0:T(8,128)S(1)}, f32[15,128]{1,0:T(8,128)S(1)}, s32[15,128]{1,0:T(8,128)S(1)}) custom-call(f32[4,48,128]{2,1,0:T(8,128)S(1)} %get-tuple-element.16.refs_0_, f32[4,48,128]{2,1,0:T(8,128)S(1)} %collective-permute-done.refs_1_, f32[2,48,128]{2,1,0:T(8,128)S(1)} %collective-permute-done.1.refs_2_, ...), custom_call_target="tpu_custom_call" | custom-call | tf_op jit(solution)/shard_map/pallas_call | solution.py:127
  13.0 1.6 %collective-permute-start.4 = (f32[2,15,128]{2,1,0:T(8,128)S(1)}, f32[2,15,128]{2,1,0:T(8,128)S(1)}, u32[]{:S(2)}, u32[]{:S(2)}) collective-permute-start(f32[2,15,128]{2,1,0:T(8,128)S(1)} %get-tuple-element.19), channel_id=1, source_target_pairs={{0,8},{8,0},{16,24},{24,16},{1,9},{9,1},{17,25},{25,17},{2,10},{10... | collective-permute-start | bytes 46088 | tf_op jit(solution)/shard_map/ppermute | solution.py:181
  14.7 2.2 %collective-permute-done.4 = f32[2,15,128]{2,1,0:T(8,128)S(1)} collective-permute-done((f32[2,15,128]{2,1,0:T(8,128)S(1)}, f32[2,15,128]{2,1,0:T(8,128)S(1)}, u32[]{:S(2)}, u32[]{:S(2)}) %collective-permute-start.4) | collective-permute-done | bytes 15392 | tf_op jit(solution)/shard_map/ppermute | solution.py:181
  16.9 2.8 %collective-permute-start.5 = (f32[2,15,128]{2,1,0:T(8,128)S(1)}, f32[2,15,128]{2,1,0:T(8,128)S(1)}, u32[]{:S(2)}, u32[]{:S(2)}) collective-permute-start(f32[2,15,128]{2,1,0:T(8,128)S(1)} %pad_maximum_fusion.3.mine_ref), channel_id=1, source_target_pairs={{0,16},{8,24},{16,0},{24,8},{1,17},{9,25},{17,1},{25,9},{2,18},{10... | collective-permute-start | bytes 46088 | tf_op jit(solution)/shard_map/ppermute | solution.py:184
  19.7 1.9 %collective-permute-done.5.theirs_ref = f32[2,15,128]{2,1,0:T(8,128)S(1)} collective-permute-done((f32[2,15,128]{2,1,0:T(8,128)S(1)}, f32[2,15,128]{2,1,0:T(8,128)S(1)}, u32[]{:S(2)}, u32[]{:S(2)}) %collective-permute-start.5) | collective-permute-done | bytes 15392 | tf_op jit(solution)/shard_map/ppermute | solution.py:184
  21.6 0.7 %shard_map.85 = (f32[10,1920]{1,0:T(8,128)}, f32[15,128]{1,0:T(8,128)}, f32[15,128]{1,0:T(8,128)}, f32[15,128]{1,0:T(8,128)}, s32[15,128]{1,0:T(8,128)}) custom-call(f32[10,1920]{1,0:T(8,128)S(1)} %get-tuple-element.18.dev_ref, f32[2,15,128]{2,1,0:T(8,128)S(1)} %pad_maximum_fusion.3.mine_ref, f32[2,15,128]{2,1,0:T(8,128)S(1)} %collective-permute-done.5.theirs_ref, ...), custom_call_target="tpu_custom_call" | custom-call | tf_op jit(solution)/shard_map/pallas_call | solution.py:186
  (7 shorter events, 0.0 us)
Async XLA Ops:
  1.7 1.5 %collective-permute-start = (f32[4,48,128]{2,1,0:T(8,128)S(1)}, f32[4,48,128]{2,1,0:T(8,128)S(1)}, u32[]{:S(2)}, u32[]{:S(2)}) collective-permute-start(f32[4,48,128]{2,1,0:T(8,128)S(1)} %get-tuple-element.17), channel_id=1, source_target_pairs={{0,1},{1,0},{2,3},{3,2},{4,5},{5,4},{6,7},{7,6},{8,9},{9,8},{10,11... | collective-permute-start | bytes 294920 | tf_op jit(solution)/shard_map/ppermute | solution.py:173
  3.2 5.9 %collective-permute-start.1 = (f32[2,48,128]{2,1,0:T(8,128)S(1)}, f32[2,48,128]{2,1,0:T(8,128)S(1)}, u32[]{:S(2)}, u32[]{:S(2)}) collective-permute-start(f32[2,48,128]{2,1,0:T(8,128)S(1)} %pad_maximum_fusion), channel_id=1, source_target_pairs={{0,6},{1,7},{2,4},{3,5},{4,2},{5,3},{6,0},{7,1},{8,14},{9,15},{10,... | collective-permute-start | bytes 147464 | tf_op jit(solution)/shard_map/ppermute | solution.py:177
  7.1 4.1 %collective-permute-start.2 = (f32[2,48,128]{2,1,0:T(8,128)S(1)}, f32[2,48,128]{2,1,0:T(8,128)S(1)}, u32[]{:S(2)}, u32[]{:S(2)}) collective-permute-start(f32[2,48,128]{2,1,0:T(8,128)S(1)} %pad_maximum_fusion.1), channel_id=1, source_target_pairs={{0,4},{1,5},{2,6},{3,7},{4,0},{5,1},{6,2},{7,3},{8,12},{9,13},{10,... | collective-permute-start | bytes 147464 | tf_op jit(solution)/shard_map/ppermute | solution.py:177
  7.6 4.1 %collective-permute-start.3 = (f32[2,48,128]{2,1,0:T(8,128)S(1)}, f32[2,48,128]{2,1,0:T(8,128)S(1)}, u32[]{:S(2)}, u32[]{:S(2)}) collective-permute-start(f32[2,48,128]{2,1,0:T(8,128)S(1)} %pad_maximum_fusion.2), channel_id=1, source_target_pairs={{0,2},{1,3},{2,0},{3,1},{4,6},{5,7},{6,4},{7,5},{8,10},{9,11},{10,... | collective-permute-start | bytes 147464 | tf_op jit(solution)/shard_map/ppermute | solution.py:177
  13.0 3.8 %collective-permute-start.4 = (f32[2,15,128]{2,1,0:T(8,128)S(1)}, f32[2,15,128]{2,1,0:T(8,128)S(1)}, u32[]{:S(2)}, u32[]{:S(2)}) collective-permute-start(f32[2,15,128]{2,1,0:T(8,128)S(1)} %get-tuple-element.19), channel_id=1, source_target_pairs={{0,8},{8,0},{16,24},{24,16},{1,9},{9,1},{17,25},{25,17},{2,10},{10... | collective-permute-start | bytes 46088 | tf_op jit(solution)/shard_map/ppermute | solution.py:181
  16.9 4.7 %collective-permute-start.5 = (f32[2,15,128]{2,1,0:T(8,128)S(1)}, f32[2,15,128]{2,1,0:T(8,128)S(1)}, u32[]{:S(2)}, u32[]{:S(2)}) collective-permute-start(f32[2,15,128]{2,1,0:T(8,128)S(1)} %pad_maximum_fusion.3.mine_ref), channel_id=1, source_target_pairs={{0,16},{8,24},{16,0},{24,8},{1,17},{9,25},{17,1},{25,9},{2,18},{10... | collective-permute-start | bytes 46088 | tf_op jit(solution)/shard_map/ppermute | solution.py:184

commit v2 on v1

--- a/solution.py
+++ b/solution.py
@@ -26,7 +26,7 @@
     rest = rows - whole
     for step in range(regions):
         owner = me ^ step
-        out_ref = other_ref if step % 2 else same_ref
+        out_ref = other_ref if (step % 2) ^ (step > 1) else same_ref
         for j in range(chunks):
             line = owner * chunks + j
             values = value_ref[:, pl.ds(pl.multiple_of(line * LANES, LANES), LANES)]
@@ -42,7 +42,7 @@
             out_ref[step // 2, pl.ds(tail + members - whole + 1, 1), :] = local
 
 
-def bin_kernel(members, chunks, groups, in_refs, dev_ref, moment_ref, error_ref, count_ref, acc_ref):
+def accumulate(members, chunks, groups, in_refs, start_ref, acc_ref):
     rows, whole = block_rows(members)
     rest = rows - whole
     pad = round_up(rows, 16)
@@ -81,10 +81,16 @@
         product = lax.dot_general(
             left, low, (((1,), (1,)), ((), ())), preferred_element_type=jnp.float32
         )
-        if n == 0:
+        if n == 0 and start_ref is None:
             acc_ref[...] = product
+        elif n == 0:
+            acc_ref[...] = start_ref[...] + product
         else:
             acc_ref[...] += product
+
+
+def finish(members, groups, acc_ref, dev_ref, moment_ref, error_ref, count_ref):
+    pad = round_up(block_rows(members)[0], 16)
     for g in range(groups):
         start, width = g * WIDE, min(WIDE, CELL_DEV - g * WIDE)
         base = g * 3 * pad
@@ -115,15 +121,21 @@
     return pltpu.with_memory_space_constraint(array, pltpu.VMEM)
 
 
-def bin_call(members, chunks, arrays):
+def bin_some(members, chunks, arrays, start=None, last=False):
     groups = -(-CELL_DEV // WIDE)
     pad = round_up(block_rows(members)[0], 16)
+    lines = CELL_DEV // LANES
+    acc = pltpu.VMEM((groups * 3 * pad, WIDE), jnp.float32)
+    inputs = [array for array, _ in arrays] + ([] if start is None else [start])
 
     def body(*refs):
-        pairs = list(zip(refs, [picks for _, picks in arrays]))
-        bin_kernel(members, chunks, groups, pairs, *refs[len(arrays) :])
-
-    lines = CELL_DEV // LANES
+        ins, outs = refs[: len(inputs)], refs[len(inputs) :]
+        start_ref = None if start is None else ins[-1]
+        pairs = list(zip(ins, [picks for _, picks in arrays]))
+        accumulate(members, chunks, groups, pairs, start_ref, outs[-1])
+        if last:
+            finish(members, groups, outs[-1], *outs[:-1])
+
     return pl.pallas_call(
         body,
         out_shape=[
@@ -131,9 +143,11 @@
             pltpu.VMEM((2, lines, LANES), jnp.float32),
             pltpu.VMEM((lines, LANES), jnp.float32),
             pltpu.VMEM((lines, LANES), jnp.int32),
-        ],
-        scratch_shapes=[pltpu.VMEM((groups * 3 * pad, WIDE), jnp.float32)],
-    )(*[near(array) for array, _ in arrays])
+        ]
+        if last
+        else acc,
+        scratch_shapes=[acc] if last else [],
+    )(*[near(array) for array in inputs])
 
 
 def final_kernel(
@@ -158,7 +172,11 @@
     return jnp.stack([mine[0] + theirs[0], mine[1] + theirs[1] + gap * gap / (2 * each)])
 
 
-def shards(member_values, obs_value, obs_weight, obs_cell):
+def chip_order(chips):
+    return list(range(chips - 1, 0, -1))
+
+
+def step(member_values, obs_value, obs_weight, obs_cell):
     regions = lax.axis_size("reg")
     groups = lax.axis_size("mem")
     members, slots = member_values.shape
@@ -171,11 +189,16 @@
         out_shape=[pltpu.VMEM((chips, chunks * block_rows(members)[0], LANES), jnp.float32)] * 2,
     )(member_values, obs_value.reshape(lines), obs_weight.reshape(lines), obs_cell.reshape(lines))
     partner = lax.ppermute(other, "reg", [(i, i ^ 1) for i in range(regions)])
-    arrays = [(same, (0,)), (partner, (0,))]
-    for k in range(chips - 1, 0, -1):
+    local = [(same, (0,)), (partner, (0,))]
+    order = chip_order(chips)
+    arrivals = []
+    for k in order:
         sent = jnp.stack([same[k], partner[k]])
-        arrays.append((lax.ppermute(sent, "reg", [(i, i ^ (2 * k)) for i in range(regions)]), (0, 1)))
-    deviation, moments, error_variance, obs_total = bin_call(members, chunks, arrays)
+        arrivals.append((lax.ppermute(sent, "reg", [(i, i ^ (2 * k + 1)) for i in range(regions)]), (0, 1)))
+    sums = None
+    for n, arrival in enumerate(arrivals):
+        sums = bin_some(members, chunks, local * (n == 0) + [arrival], sums, n == chips - 2)
+    deviation, moments, error_variance, obs_total = sums
     each, reach = members, 1
     while 2 * reach < groups:
         theirs = lax.ppermute(moments, "mem", [(i, i ^ reach) for i in range(groups)])
@@ -192,7 +215,7 @@
 
 def solution(mesh):
     return jax.shard_map(
-        shards,
+        step,
         mesh=mesh,
         in_specs=(P("mem", "reg"), P("reg"), P("reg"), P("reg")),
         out_specs=(P("mem", "reg"), P("reg"), P("reg"), P("reg"), P("reg")),

time: 22.4 us -> 21.2 us (0.946)
  waiting for transfers between devices: 8.95 us -> 8.03 us
  starting transfers between devices: 9.5 us -> 9.06 us
    ppermute x6, waiting for transfers between devices: 8.95 us -> 8.03 us  [the longest x2 4.21 us: step(): lax.ppermute(moments, 'mem', [(i, i ^ reach) for i in range(groups)])]
    ppermute x6, starting transfers between devices: 9.5 us -> 9.06 us  [the longest x2 4.3 us: step(): lax.ppermute(moments, 'mem', [(i, i ^ reach) for i in range(groups)])]
    pallas_call x3 -> x5, Pallas kernels: 3.1 us -> 3.26 us  [the longest x3 1.54 us: bin_some(): pl.pallas_call(body, out_shape=[pltpu.VMEM((members, CELL_DEV), jnp.float...]
  transfers between devices with their start and end apart: 6 -> 6, of which waited for: 6 -> 4; matrix products, arithmetic and copies ran while one was open for 0% -> 0% of each run, Pallas kernels for 0% -> 5%
where the time goes in v2:
time: 21.2 us; the launch traced here: 21.1 us
  starting transfers between devices  9.06 us (43%)
  waiting for transfers between devices  8.03 us (38%)
  Pallas kernels  3.26 us (15%)
  between operations  0.68 us (3%)
    ppermute x2, starting transfers between devices, step(): lax.ppermute(moments, 'mem', [(i, i ^ reach) for i in range(groups)])  4.3 us
    ppermute x3, starting transfers between devices, step(): lax.ppermute(sent, 'reg', [(i, i ^ 2 * k + 1) for i in range(regions)])  4.21 us
    ppermute x2, waiting for transfers between devices, step(): lax.ppermute(moments, 'mem', [(i, i ^ reach) for i in range(groups)])  4.21 us
    ppermute x3, waiting for transfers between devices, step(): lax.ppermute(sent, 'reg', [(i, i ^ 2 * k + 1) for i in range(regions)])  2.89 us
    pallas_call x3, Pallas kernels, bin_some(): pl.pallas_call(body, out_shape=[pltpu.VMEM((members, CELL_DEV), jnp.float...  1.54 us
    pallas_call x1, Pallas kernels, step(): pl.pallas_call(functools.partial(pack_kernel, members, regions, chunks),...  1.05 us
    ppermute x1, waiting for transfers between devices, step(): partner = lax.ppermute(other, 'reg', [(i, i ^ 1) for i in range(regions)])  0.94 us
    pallas_call x1, Pallas kernels, step(): pl.pallas_call(functools.partial(final_kernel, members * groups), out_sha...  0.67 us
  transfers between devices with their start and end apart: 6, of which 4 were waited for; matrix products, arithmetic and copies ran while one was open for 0% of the time, Pallas kernels for 5%

profile of v2, /device:TPU:0, one launch (start us, length us, event | category | flops | bytes accessed | tf_op | source)
XLA Modules:
  0.0 21.1 jit_solution(9781054563262185125)
XLA Ops:
  0.6 1.1 %shard_map.83 = (f32[4,48,128]{2,1,0:T(8,128)S(1)}, f32[4,48,128]{2,1,0:T(8,128)S(1)}) custom-call(f32[10,4096]{1,0:T(8,128)} %value_ref.1, f32[32,128]{1,0:T(8,128)} %bitcast.7, f32[32,128]{1,0:T(8,128)} %bitcast.8, s32[32,128]{1,0:T(8,128)} %bitcast.9), custom_call_target="tpu_custom_call" | custom-call | tf_op jit(solution)/shard_map/pallas_call | solution.py:187
  1.7 0.6 %collective-permute-start = (f32[4,48,128]{2,1,0:T(8,128)S(1)}, f32[4,48,128]{2,1,0:T(8,128)S(1)}, u32[]{:S(2)}, u32[]{:S(2)}) collective-permute-start(f32[4,48,128]{2,1,0:T(8,128)S(1)} %get-tuple-element.17), channel_id=1, source_target_pairs={{0,1},{1,0},{2,3},{3,2},{4,5},{5,4},{6,7},{7,6},{8,9},{9,8},{10,11... | collective-permute-start | bytes 294920 | tf_op jit(solution)/shard_map/ppermute | solution.py:191
  2.2 0.9 %collective-permute-done.refs_1_ = f32[4,48,128]{2,1,0:T(8,128)S(1)} collective-permute-done((f32[4,48,128]{2,1,0:T(8,128)S(1)}, f32[4,48,128]{2,1,0:T(8,128)S(1)}, u32[]{:S(2)}, u32[]{:S(2)}) %collective-permute-start) | collective-permute-done | bytes 98336 | tf_op jit(solution)/shard_map/ppermute | solution.py:191
  3.2 2.7 %collective-permute-start.2 = (f32[2,48,128]{2,1,0:T(8,128)S(1)}, f32[2,48,128]{2,1,0:T(8,128)S(1)}, u32[]{:S(2)}, u32[]{:S(2)}) collective-permute-start(f32[2,48,128]{2,1,0:T(8,128)S(1)} %pad_maximum_fusion.1), channel_id=1, source_target_pairs={{0,5},{1,4},{2,7},{3,6},{4,1},{5,0},{6,3},{7,2},{8,13},{9,12},{10,... | collective-permute-start | bytes 147464 | tf_op jit(solution)/shard_map/ppermute | solution.py:197
  5.9 1.4 %collective-permute-start.3 = (f32[2,48,128]{2,1,0:T(8,128)S(1)}, f32[2,48,128]{2,1,0:T(8,128)S(1)}, u32[]{:S(2)}, u32[]{:S(2)}) collective-permute-start(f32[2,48,128]{2,1,0:T(8,128)S(1)} %pad_maximum_fusion.2), channel_id=1, source_target_pairs={{0,7},{1,6},{2,5},{3,4},{4,3},{5,2},{6,1},{7,0},{8,15},{9,14},{10,... | collective-permute-start | bytes 147464 | tf_op jit(solution)/shard_map/ppermute | solution.py:197
  7.3 0.1 collective-permute-start.1
  7.4 2.9 %collective-permute-done.3.refs_2_ = f32[2,48,128]{2,1,0:T(8,128)S(1)} collective-permute-done((f32[2,48,128]{2,1,0:T(8,128)S(1)}, f32[2,48,128]{2,1,0:T(8,128)S(1)}, u32[]{:S(2)}, u32[]{:S(2)}) %collective-permute-start.3) | collective-permute-done | bytes 49184 | tf_op jit(solution)/shard_map/ppermute | solution.py:197
  10.3 0.6 %shard_map.84.refs_1_ = f32[384,256]{1,0:T(8,128)S(1)} custom-call(f32[4,48,128]{2,1,0:T(8,128)S(1)} %get-tuple-element.16.refs_0_, f32[4,48,128]{2,1,0:T(8,128)S(1)} %collective-permute-done.refs_1_, f32[2,48,128]{2,1,0:T(8,128)S(1)} %collective-permute-done.3.refs_2_), custom_call_target="tpu_custom_call" | custom-call | tf_op jit(solution)/shard_map/pallas_call | solution.py:139
  10.9 0.0 collective-permute-done.2.refs_0_
  10.9 0.4 %shard_map.85.refs_1_ = f32[384,256]{1,0:T(8,128)S(1)} custom-call(f32[2,48,128]{2,1,0:T(8,128)S(1)} %collective-permute-done.2.refs_0_, f32[384,256]{1,0:T(8,128)S(1)} %shard_map.84.refs_1_), custom_call_target="tpu_custom_call" | custom-call | tf_op jit(solution)/shard_map/pallas_call | solution.py:139
  11.4 0.0 collective-permute-done.1.refs_0_
  11.4 0.5 %shard_map.86 = (f32[10,1920]{1,0:T(8,128)S(1)}, f32[2,15,128]{2,1,0:T(8,128)S(1)}, f32[15,128]{1,0:T(8,128)S(1)}, s32[15,128]{1,0:T(8,128)S(1)}) custom-call(f32[2,48,128]{2,1,0:T(8,128)S(1)} %collective-permute-done.1.refs_0_, f32[384,256]{1,0:T(8,128)S(1)} %shard_map.85.refs_1_), custom_call_target="tpu_custom_call" | custom-call | tf_op jit(solution)/shard_map/pallas_call | solution.py:139
  11.9 1.6 %collective-permute-start.4 = (f32[2,15,128]{2,1,0:T(8,128)S(1)}, f32[2,15,128]{2,1,0:T(8,128)S(1)}, u32[]{:S(2)}, u32[]{:S(2)}) collective-permute-start(f32[2,15,128]{2,1,0:T(8,128)S(1)} %get-tuple-element.19), channel_id=1, source_target_pairs={{0,8},{8,0},{16,24},{24,16},{1,9},{9,1},{17,25},{25,17},{2,10},{10... | collective-permute-start | bytes 46088 | tf_op jit(solution)/shard_map/ppermute | solution.py:204
  13.5 2.2 %collective-permute-done.4 = f32[2,15,128]{2,1,0:T(8,128)S(1)} collective-permute-done((f32[2,15,128]{2,1,0:T(8,128)S(1)}, f32[2,15,128]{2,1,0:T(8,128)S(1)}, u32[]{:S(2)}, u32[]{:S(2)}) %collective-permute-start.4) | collective-permute-done | bytes 15392 | tf_op jit(solution)/shard_map/ppermute | solution.py:204
  15.7 2.7 %collective-permute-start.5 = (f32[2,15,128]{2,1,0:T(8,128)S(1)}, f32[2,15,128]{2,1,0:T(8,128)S(1)}, u32[]{:S(2)}, u32[]{:S(2)}) collective-permute-start(f32[2,15,128]{2,1,0:T(8,128)S(1)} %pad_maximum_fusion.3.mine_ref), channel_id=1, source_target_pairs={{0,16},{8,24},{16,0},{24,8},{1,17},{9,25},{17,1},{25,9},{2,18},{10... | collective-permute-start | bytes 46088 | tf_op jit(solution)/shard_map/ppermute | solution.py:207
  18.4 2.0 %collective-permute-done.5.theirs_ref = f32[2,15,128]{2,1,0:T(8,128)S(1)} collective-permute-done((f32[2,15,128]{2,1,0:T(8,128)S(1)}, f32[2,15,128]{2,1,0:T(8,128)S(1)}, u32[]{:S(2)}, u32[]{:S(2)}) %collective-permute-start.5) | collective-permute-done | bytes 15392 | tf_op jit(solution)/shard_map/ppermute | solution.py:207
  20.4 0.7 %shard_map.87 = (f32[10,1920]{1,0:T(8,128)}, f32[15,128]{1,0:T(8,128)}, f32[15,128]{1,0:T(8,128)}, f32[15,128]{1,0:T(8,128)}, s32[15,128]{1,0:T(8,128)}) custom-call(f32[10,1920]{1,0:T(8,128)S(1)} %get-tuple-element.18.dev_ref, f32[2,15,128]{2,1,0:T(8,128)S(1)} %pad_maximum_fusion.3.mine_ref, f32[2,15,128]{2,1,0:T(8,128)S(1)} %collective-permute-done.5.theirs_ref, ...), custom_call_target="tpu_custom_call" | custom-call | tf_op jit(solution)/shard_map/pallas_call | solution.py:209
  (7 shorter events, 0.0 us)
Async XLA Ops:
  1.7 1.5 %collective-permute-start = (f32[4,48,128]{2,1,0:T(8,128)S(1)}, f32[4,48,128]{2,1,0:T(8,128)S(1)}, u32[]{:S(2)}, u32[]{:S(2)}) collective-permute-start(f32[4,48,128]{2,1,0:T(8,128)S(1)} %get-tuple-element.17), channel_id=1, source_target_pairs={{0,1},{1,0},{2,3},{3,2},{4,5},{5,4},{6,7},{7,6},{8,9},{9,8},{10,11... | collective-permute-start | bytes 294920 | tf_op jit(solution)/shard_map/ppermute | solution.py:191
  3.2 7.7 %collective-permute-start.2 = (f32[2,48,128]{2,1,0:T(8,128)S(1)}, f32[2,48,128]{2,1,0:T(8,128)S(1)}, u32[]{:S(2)}, u32[]{:S(2)}) collective-permute-start(f32[2,48,128]{2,1,0:T(8,128)S(1)} %pad_maximum_fusion.1), channel_id=1, source_target_pairs={{0,5},{1,4},{2,7},{3,6},{4,1},{5,0},{6,3},{7,2},{8,13},{9,12},{10,... | collective-permute-start | bytes 147464 | tf_op jit(solution)/shard_map/ppermute | solution.py:197
  5.9 4.4 %collective-permute-start.3 = (f32[2,48,128]{2,1,0:T(8,128)S(1)}, f32[2,48,128]{2,1,0:T(8,128)S(1)}, u32[]{:S(2)}, u32[]{:S(2)}) collective-permute-start(f32[2,48,128]{2,1,0:T(8,128)S(1)} %pad_maximum_fusion.2), channel_id=1, source_target_pairs={{0,7},{1,6},{2,5},{3,4},{4,3},{5,2},{6,1},{7,0},{8,15},{9,14},{10,... | collective-permute-start | bytes 147464 | tf_op jit(solution)/shard_map/ppermute | solution.py:197
  7.3 4.1 %collective-permute-start.1 = (f32[2,48,128]{2,1,0:T(8,128)S(1)}, f32[2,48,128]{2,1,0:T(8,128)S(1)}, u32[]{:S(2)}, u32[]{:S(2)}) collective-permute-start(f32[2,48,128]{2,1,0:T(8,128)S(1)} %pad_maximum_fusion), channel_id=1, source_target_pairs={{0,3},{1,2},{2,1},{3,0},{4,7},{5,6},{6,5},{7,4},{8,11},{9,10},{10,... | collective-permute-start | bytes 147464 | tf_op jit(solution)/shard_map/ppermute | solution.py:197
  11.9 3.8 %collective-permute-start.4 = (f32[2,15,128]{2,1,0:T(8,128)S(1)}, f32[2,15,128]{2,1,0:T(8,128)S(1)}, u32[]{:S(2)}, u32[]{:S(2)}) collective-permute-start(f32[2,15,128]{2,1,0:T(8,128)S(1)} %get-tuple-element.19), channel_id=1, source_target_pairs={{0,8},{8,0},{16,24},{24,16},{1,9},{9,1},{17,25},{25,17},{2,10},{10... | collective-permute-start | bytes 46088 | tf_op jit(solution)/shard_map/ppermute | solution.py:204
  15.7 4.7 %collective-permute-start.5 = (f32[2,15,128]{2,1,0:T(8,128)S(1)}, f32[2,15,128]{2,1,0:T(8,128)S(1)}, u32[]{:S(2)}, u32[]{:S(2)}) collective-permute-start(f32[2,15,128]{2,1,0:T(8,128)S(1)} %pad_maximum_fusion.3.mine_ref), channel_id=1, source_target_pairs={{0,16},{8,24},{16,0},{24,8},{1,17},{9,25},{17,1},{25,9},{2,18},{10... | collective-permute-start | bytes 46088 | tf_op jit(solution)/shard_map/ppermute | solution.py:207

commit v3 on v0

v3 whole, which is shorter than its diff:
```python
import functools
import jax
import jax.numpy as jnp
from jax import lax
from jax.experimental import pallas as pl
from jax.experimental.pallas import tpu as pltpu
from jax.sharding import PartitionSpec as P

CELL_DEV = 1920
LANES = 128
WIDE = 256
LINES = CELL_DEV // LANES
GROUPS = -(-CELL_DEV // WIDE)


def round_up(size, unit):
    return -(-size // unit) * unit


def block_rows(members):
    rows = round_up(members + 2, 4)
    return rows, rows // 8 * 8


def pack_kernel(members, chips, chunks, value_ref, obs_ref, weight_ref, cell_ref, out_ref):
    chip = lax.axis_index("reg") // 2
    rows, whole = block_rows(members)
    rest = rows - whole
    for step in range(chips):
        for core in range(2):
            owner = (chip ^ step) * 2 + core
            for j in range(chunks):
                line = owner * chunks + j
                values = value_ref[:, pl.ds(pl.multiple_of(line * LANES, LANES), LANES)]
                cell = cell_ref[pl.ds(line, 1), :]
                live = cell >= 0
                weight = jnp.where(live, weight_ref[pl.ds(line, 1), :], 0.0)
                local = jnp.where(live, cell - owner * CELL_DEV, -1).astype(jnp.float32)
                innovation = (values - obs_ref[pl.ds(line, 1), :]) * weight
                tail = whole * chunks + j * rest
                out_ref[step, core, pl.ds(j * whole, whole), :] = innovation[:whole]
                out_ref[step, core, pl.ds(tail, members - whole), :] = innovation[whole:]
                out_ref[step, core, pl.ds(tail + members - whole, 1), :] = weight
                out_ref[step, core, pl.ds(tail + members - whole + 1, 1), :] = local


def split(values):
    top = values.astype(jnp.bfloat16).astype(jnp.float32)
    return top, (values - top).astype(jnp.bfloat16).astype(jnp.float32)


def accumulate(members, chunks, in_refs, start_ref, acc_ref):
    rows, whole = block_rows(members)
    rest = rows - whole
    height = GROUPS * 2 * rows
    low_iota = lax.broadcasted_iota(jnp.int32, (WIDE, LANES), 0)
    low_half = low_iota.astype(jnp.float32).astype(jnp.bfloat16)
    one, nil = jnp.ones((), jnp.bfloat16), jnp.zeros((), jnp.bfloat16)
    row_iota = lax.broadcasted_iota(jnp.int32, (2 * rest, LANES), 0)
    blocks = [(core, ref, b) for core in range(2) for ref, picks in in_refs for b in picks]
    seen = set()
    for core, ref, b in blocks:
        pieces, lows = [], []
        for j in range(chunks):
            tail = whole * chunks + j * rest
            main_top, main_rest = split(ref[b, core, pl.ds(j * whole, whole), :])
            end = ref[b, core, pl.ds(tail, rest), :]
            cell = end[members - whole + 1 : members - whole + 2].astype(jnp.int32)
            live = (cell >= 0).astype(jnp.float32)
            end = jnp.concatenate([end, end], 0)
            end = jnp.where(row_iota % rest == members - whole + 1, live, end)
            end_top, end_rest = split(end)
            end = jnp.where(row_iota < rest, end_top, end_rest)
            piece = jnp.concatenate([main_top, main_rest, end], 0)
            high = lax.shift_right_arithmetic(cell, 8)
            pieces.append([jnp.where(high == g, piece, 0.0) for g in range(GROUPS)])
            lows.append(jnp.where(low_half == (cell & (WIDE - 1)).astype(jnp.float32).astype(jnp.bfloat16), one, nil))
        left = jnp.concatenate(
            [jnp.concatenate([p[g] for p in pieces], 1) for g in range(GROUPS)], 0
        ).astype(jnp.bfloat16)
        low = jnp.concatenate(lows, 1)
        product = lax.dot_general(
            left, low, (((1,), (1,)), ((), ())), preferred_element_type=jnp.float32
        )
        spot = pl.ds(core * height, height)
        if core in seen:
            acc_ref[spot, :] += product
        elif start_ref is None:
            acc_ref[spot, :] = product
        else:
            acc_ref[spot, :] = start_ref[spot, :] + product
        seen.add(core)


def finish(members, acc_ref, moment_ref, *result_refs):
    rows, whole = block_rows(members)
    rest, extra = rows - whole, members - whole
    for core, result_ref in enumerate(result_refs):
        for g in range(GROUPS):
            start, width = g * WIDE, min(WIDE, CELL_DEV - g * WIDE)
            base = (core * GROUPS + g) * 2 * rows
            main = acc_ref[pl.ds(base, whole), :width] + acc_ref[pl.ds(base + whole, whole), :width]
            end = acc_ref[pl.ds(base + 2 * whole, 2 * rest), :width]
            end = end[:rest] + end[rest:]
            counted = end[extra + 1 : extra + 2]
            filled = counted > 0
            total = jnp.where(filled, end[extra : extra + 1], 1.0)
            inverse = 1.0 / total
            main = main * inverse
            last = end[:extra] * inverse
            moment = jnp.sum(main, 0, keepdims=True) + jnp.sum(last, 0, keepdims=True)
            mean = moment * (1.0 / members)
            main_gap, last_gap = main - mean, last - mean
            spread = jnp.sum(main_gap * main_gap, 0, keepdims=True) + jnp.sum(last_gap * last_gap, 0, keepdims=True)
            result_ref[:whole, start : start + width] = main
            result_ref[whole:members, start : start + width] = last
            result_ref[members : members + 1, start : start + width] = jnp.where(filled, inverse, 0.0)
            result_ref[members + 1 : members + 2, start : start + width] = counted
            for j in range(width // LANES):
                line, cut = start // LANES + j, slice(j * LANES, (j + 1) * LANES)
                moment_ref[core, 0, line : line + 1, :] = moment[:, cut]
                moment_ref[core, 1, line : line + 1, :] = spread[:, cut]


def near(array):
    return pltpu.with_memory_space_constraint(array, pltpu.VMEM)


def bin_some(members, chunks, arrays, start=None, last=False):
    acc = pltpu.VMEM((2 * GROUPS * 2 * block_rows(members)[0], WIDE), jnp.float32)
    inputs = [array for array, _ in arrays] + ([] if start is None else [start])

    def body(*refs):
        ins, outs = refs[: len(inputs)], refs[len(inputs) :]
        start_ref = None if start is None else ins[-1]
        pairs = list(zip(ins, [picks for _, picks in arrays]))
        accumulate(members, chunks, pairs, start_ref, outs[-1])
        if last:
            finish(members, outs[-1], *outs[:-1])

    return pl.pallas_call(
        body,
        out_shape=[pltpu.VMEM((2, 2, LINES, LANES), jnp.float32)]
        + [pltpu.VMEM((members + 2, CELL_DEV), jnp.float32)] * 2
        if last
        else acc,
        scratch_shapes=[acc] if last else [],
    )(*[near(array) for array in inputs])


def final_kernel(
    members, total, own_ref, passed_ref, moment_ref, far_ref, out_ref, departure_ref, variance_ref, error_ref, count_ref
):
    def write(core, result_ref, merged_ref):
        mean = merged_ref[core, 0] * (1.0 / total)
        departure_ref[...] = -mean
        variance_ref[...] = merged_ref[core, 1] * (1.0 / (total - 1))
        for j in range(LINES):
            cut = slice(j * LANES, (j + 1) * LANES)
            out_ref[:, cut] = result_ref[:members, cut] - mean[j : j + 1]
            error_ref[j : j + 1, :] = result_ref[members : members + 1, cut]
            count_ref[j : j + 1, :] = result_ref[members + 1 : members + 2, cut].astype(jnp.int32)

    core = lax.axis_index("reg") % 2
    pl.when(core == 1)(lambda: write(1, own_ref, moment_ref))
    pl.when(core == 0)(lambda: write(0, passed_ref, far_ref))


def merge(mine, theirs, each):
    gap = mine[:, 0] - theirs[:, 0]
    spread = mine[:, 1] + theirs[:, 1] + gap * gap / (2 * each)
    return jnp.stack([mine[:, 0] + theirs[:, 0], spread], 1)


def chip_order(chips):
    return list(range(chips - 1, 0, -1))


def idle(members, packed, partner):
    shape = (members + 2, CELL_DEV)
    return jnp.zeros((2, 2, LINES, LANES)), jnp.zeros(shape), jnp.zeros(shape)


def hub(members, chunks, regions, packed, partner):
    chips = regions // 2
    arrivals = []
    for k in chip_order(chips):
        sent = jnp.stack([packed[k], partner[k]])
        pairs = [(i, i ^ (2 * k)) for i in range(regions)]
        arrivals.append((lax.ppermute(sent, "reg", pairs), (0, 1)))
    sums = bin_some(members, chunks, [(packed, (0,)), (partner, (0,))])
    for n, arrival in enumerate(arrivals):
        sums = bin_some(members, chunks, [arrival], sums, n == chips - 2)
    return sums


def reduce_mem(members, groups, moments):
    each, reach = members, 1
    while reach < groups:
        theirs = lax.ppermute(moments, "mem", [(z, z ^ reach) for z in range(groups)])
        moments = merge(moments, theirs, each)
        each, reach = 2 * each, 2 * reach
    return moments


def step(member_values, obs_value, obs_weight, obs_cell):
    regions = lax.axis_size("reg")
    groups = lax.axis_size("mem")
    members, slots = member_values.shape
    chunks = slots // regions // LANES
    chips = regions // 2
    swap = [(i, i ^ 1) for i in range(regions)]
    lines = (slots // LANES, LANES)
    packed = pl.pallas_call(
        functools.partial(pack_kernel, members, chips, chunks),
        out_shape=pltpu.VMEM((chips, 2, chunks * block_rows(members)[0], LANES), jnp.float32),
    )(member_values, obs_value.reshape(lines), obs_weight.reshape(lines), obs_cell.reshape(lines))
    partner = lax.ppermute(packed, "reg", swap)
    north = lax.axis_index("reg") % 2 == 1
    moments, passed, own = lax.cond(
        north, functools.partial(hub, members, chunks, regions), functools.partial(idle, members), packed, partner
    )
    passed = lax.ppermute(passed, "reg", swap)
    moments = lax.cond(north, functools.partial(reduce_mem, members, groups), lambda m: m, moments)
    far = lax.ppermute(moments, "reg", swap)
    cells = jax.ShapeDtypeStruct((LINES, LANES), jnp.float32)
    outs = pl.pallas_call(
        functools.partial(final_kernel, members, members * groups),
        out_shape=[
            jax.ShapeDtypeStruct((members, CELL_DEV), jnp.float32),
            cells,
            cells,
            cells,
            jax.ShapeDtypeStruct((LINES, LANES), jnp.int32),
        ],
    )(*[near(a) for a in (own, passed, moments, far)])
    return (outs[0], *[out.reshape(-1) for out in outs[1:]])


def solution(mesh):
    return jax.shard_map(
        step,
        mesh=mesh,
        in_specs=(P("mem", "reg"), P("reg"), P("reg"), P("reg")),
        out_specs=(P("mem", "reg"), P("reg"), P("reg"), P("reg"), P("reg")),
        check_vma=False,
    )
```

time: 49 us -> 20.8 us (0.42)
  blocking collectives: 19 us -> 0 us
  starting transfers between devices: 5.2 us -> 16.3 us
  matrix products: 10.3 us -> 0 us
  waiting for transfers between devices: 6.9 us -> 1.93 us
  other arithmetic: 4.73 us -> 0 us
  Pallas kernels: 0 us -> 1.74 us
  local copies, waits for them, and re-layouts: 1.52 us -> 0.02 us
    psum x1 -> x0, blocking collectives: 19 us -> none  [shards(): lax.psum((jnp.sum(superob, 0), jnp.sum(superob * superob, 0)), 'mem')]
    ppermute x0 -> x3, starting transfers between devices: none -> 16.3 us  [the longest x1 9.04 us: step(): passed = lax.ppermute(passed, 'reg', swap)]
    dot_general x4 -> x0, matrix products: 10.3 us -> none  [add_block(): jnp.dot(block_columns, one_hot, precision=lax.Precision.HIGHEST, preferre...]
    all_to_all x1 -> x0, waiting for transfers between devices: 6.9 us -> none  [shards(): lax.all_to_all(payload, 'reg', split_axis=1, concat_axis=1, tiled=True)]
    all_to_all x1 -> x0, starting transfers between devices: 5.2 us -> none  [shards(): lax.all_to_all(payload, 'reg', split_axis=1, concat_axis=1, tiled=True)]
    ppermute x0 -> x3, waiting for transfers between devices: none -> 1.93 us  [the longest x1 1.07 us: step(): partner = lax.ppermute(packed, 'reg', swap)]
    pallas_call x0 -> x2, Pallas kernels: none -> 1.74 us  [the longest x1 1.05 us: step(): pl.pallas_call(functools.partial(pack_kernel, members, chips, chunks), ou...]
    mul x2 -> x0, other arithmetic: 1.73 us -> none  [the longest x1 0.97 us: shards(): weighted_members = member_values * weight[None, :]]
  transfers between devices with their start and end apart: 1 -> 3, of which waited for: 1 -> 2; matrix products, arithmetic and copies ran while one was open for 0% -> 0% of each run, Pallas kernels for 0% -> 0%
where the time goes in v3:
time: 20.8 us; the launch traced here: 20.7 us
  starting transfers between devices  16.3 us (78%)
  waiting for transfers between devices  1.93 us (9%)
  Pallas kernels  1.74 us (8%)
  between operations  0.65 us (3%)
    ppermute x1, starting transfers between devices, step(): passed = lax.ppermute(passed, 'reg', swap)  9.04 us
    ppermute x1, starting transfers between devices, step(): far = lax.ppermute(moments, 'reg', swap)  6.71 us
    ppermute x1, waiting for transfers between devices, step(): partner = lax.ppermute(packed, 'reg', swap)  1.07 us
    pallas_call x1, Pallas kernels, step(): pl.pallas_call(functools.partial(pack_kernel, members, chips, chunks), ou...  1.05 us
    ppermute x1, waiting for transfers between devices, step(): far = lax.ppermute(moments, 'reg', swap)  0.86 us
    pallas_call x1, Pallas kernels, step(): pl.pallas_call(functools.partial(final_kernel, members, members * groups)...  0.69 us
    ppermute x1, starting transfers between devices, step(): partner = lax.ppermute(packed, 'reg', swap)  0.56 us
  transfers between devices with their start and end apart: 3, of which 2 were waited for; matrix products, arithmetic and copies ran while one was open for 0% of the time, Pallas kernels for 0%

profile of v3, /device:TPU:0, one launch (start us, length us, event | category | flops | bytes accessed | tf_op | source)
XLA Modules:
  0.0 20.7 jit_solution(4369695183315140667)
XLA Ops:
  0.6 1.1 %shard_map.83 = f32[4,2,48,128]{3,2,1,0:T(8,128)S(1)} custom-call(f32[10,4096]{1,0:T(8,128)} %value_ref.1, f32[32,128]{1,0:T(8,128)} %bitcast.7, f32[32,128]{1,0:T(8,128)} %bitcast.8, s32[32,128]{1,0:T(8,128)} %bitcast.9), custom_call_target="tpu_custom_call" | custom-call | tf_op jit(solution)/shard_map/pallas_call | solution.py:214
  1.7 0.6 %collective-permute-start.5 = (f32[4,2,48,128]{3,2,1,0:T(8,128)S(1)}, f32[4,2,48,128]{3,2,1,0:T(8,128)S(1)}, u32[]{:S(2)}, u32[]{:S(2)}) collective-permute-start(f32[4,2,48,128]{3,2,1,0:T(8,128)S(1)} %shard_map.83), channel_id=1, source_target_pairs={{0,1},{1,0},{2,3},{3,2},{4,5},{5,4},{6,7},{7,6},{8,9},{9,8},{10,11... | collective-permute-start | bytes 589832 | tf_op jit(solution)/shard_map/ppermute | solution.py:218
  2.2 1.1 %collective-permute-done.5 = f32[4,2,48,128]{3,2,1,0:T(8,128)S(1)} collective-permute-done((f32[4,2,48,128]{3,2,1,0:T(8,128)S(1)}, f32[4,2,48,128]{3,2,1,0:T(8,128)S(1)}, u32[]{:S(2)}, u32[]{:S(2)}) %collective-permute-start.5) | collective-permute-done | bytes 196640 | tf_op jit(solution)/shard_map/ppermute | solution.py:218
  3.4 9.0 %collective-permute-start.6 = (f32[12,1920]{1,0:T(8,128)S(1)}, f32[12,1920]{1,0:T(8,128)S(1)}, u32[]{:S(2)}, u32[]{:S(2)}) collective-permute-start(f32[12,1920]{1,0:T(8,128)S(1)} %get-tuple-element.32), channel_id=1, source_target_pairs={{0,1},{1,0},{2,3},{3,2},{4,5},{5,4},{6,7},{7,6},{8,9},{9,8},{10,11... | collective-permute-start | bytes 276488 | tf_op jit(solution)/shard_map/ppermute | solution.py:223
  12.4 6.7 %collective-permute-start.7 = (f32[2,2,15,128]{3,2,1,0:T(8,128)S(1)}, f32[2,2,15,128]{3,2,1,0:T(8,128)S(1)}, u32[]{:S(2)}, u32[]{:S(2)}) collective-permute-start(f32[2,2,15,128]{3,2,1,0:T(8,128)S(1)} %get-tuple-element.58.moment_ref), channel_id=1, source_target_pairs={{0,1},{1,0},{2,3},{3,2},{4,5},{5,4},{6,7},{7,6},{8,9},{9,8},{10,11... | collective-permute-start | bytes 92168 | tf_op jit(solution)/shard_map/ppermute | solution.py:225
  19.1 0.9 %collective-permute-done.7.far_ref = f32[2,2,15,128]{3,2,1,0:T(8,128)S(1)} collective-permute-done((f32[2,2,15,128]{3,2,1,0:T(8,128)S(1)}, f32[2,2,15,128]{3,2,1,0:T(8,128)S(1)}, u32[]{:S(2)}, u32[]{:S(2)}) %collective-permute-start.7) | collective-permute-done | bytes 30752 | tf_op jit(solution)/shard_map/ppermute | solution.py:225
  20.0 0.0 collective-permute-done.6.passed_ref
  20.0 0.7 %shard_map.84 = (f32[10,1920]{1,0:T(8,128)}, f32[15,128]{1,0:T(8,128)}, f32[15,128]{1,0:T(8,128)}, f32[15,128]{1,0:T(8,128)}, s32[15,128]{1,0:T(8,128)}) custom-call(f32[12,1920]{1,0:T(8,128)S(1)} %get-tuple-element.31.own_ref, f32[12,1920]{1,0:T(8,128)S(1)} %collective-permute-done.6.passed_ref, f32[2,2,15,128]{3,2,1,0:T(8,128)S(1)} %get-tuple-element.58.moment_ref, ...), custom_call_target="tpu_custom_call" | custom-call | tf_op jit(solution)/shard_map/pallas_call | solution.py:227
  (5 shorter events, 0.1 us)
Async XLA Ops:
  1.7 1.6 %collective-permute-start.5 = (f32[4,2,48,128]{3,2,1,0:T(8,128)S(1)}, f32[4,2,48,128]{3,2,1,0:T(8,128)S(1)}, u32[]{:S(2)}, u32[]{:S(2)}) collective-permute-start(f32[4,2,48,128]{3,2,1,0:T(8,128)S(1)} %shard_map.83), channel_id=1, source_target_pairs={{0,1},{1,0},{2,3},{3,2},{4,5},{5,4},{6,7},{7,6},{8,9},{9,8},{10,11... | collective-permute-start | bytes 589832 | tf_op jit(solution)/shard_map/ppermute | solution.py:218
  3.4 16.6 %collective-permute-start.6 = (f32[12,1920]{1,0:T(8,128)S(1)}, f32[12,1920]{1,0:T(8,128)S(1)}, u32[]{:S(2)}, u32[]{:S(2)}) collective-permute-start(f32[12,1920]{1,0:T(8,128)S(1)} %get-tuple-element.32), channel_id=1, source_target_pairs={{0,1},{1,0},{2,3},{3,2},{4,5},{5,4},{6,7},{7,6},{8,9},{9,8},{10,11... | collective-permute-start | bytes 276488 | tf_op jit(solution)/shard_map/ppermute | solution.py:223
  12.4 7.6 %collective-permute-start.7 = (f32[2,2,15,128]{3,2,1,0:T(8,128)S(1)}, f32[2,2,15,128]{3,2,1,0:T(8,128)S(1)}, u32[]{:S(2)}, u32[]{:S(2)}) collective-permute-start(f32[2,2,15,128]{3,2,1,0:T(8,128)S(1)} %get-tuple-element.58.moment_ref), channel_id=1, source_target_pairs={{0,1},{1,0},{2,3},{3,2},{4,5},{5,4},{6,7},{7,6},{8,9},{9,8},{10,11... | collective-permute-start | bytes 92168 | tf_op jit(solution)/shard_map/ppermute | solution.py:225

commit v4 on v2

v4 whole, which is shorter than its diff:
```python
import functools
import jax
import jax.numpy as jnp
from jax import lax
from jax.experimental import pallas as pl
from jax.experimental.pallas import tpu as pltpu
from jax.sharding import PartitionSpec as P

CELL_DEV = 1920
LANES = 128
WIDE = 256
LINES = CELL_DEV // LANES
GROUPS = -(-CELL_DEV // WIDE)


def round_up(size, unit):
    return -(-size // unit) * unit


def block_rows(members):
    rows = round_up(members + 2, 4)
    return rows, rows // 8 * 8


def odd_plane():
    plane = lax.axis_index("mem")
    odd = plane & 1
    for bit in range(1, lax.axis_size("mem").bit_length() - 1):
        odd = odd ^ (lax.shift_right_logical(plane, bit) & 1)
    return odd


def pack_kernel(members, regions, chunks, value_ref, obs_ref, weight_ref, cell_ref, same_ref, other_ref):
    me, odd = lax.axis_index("reg"), odd_plane()
    rows, whole = block_rows(members)
    rest = rows - whole
    for step in range(regions):
        owner = me ^ step ^ odd
        out_ref = other_ref if (step % 2) ^ (step > 1) else same_ref
        for j in range(chunks):
            line = owner * chunks + j
            values = value_ref[:, pl.ds(pl.multiple_of(line * LANES, LANES), LANES)]
            cell = cell_ref[pl.ds(line, 1), :]
            live = cell >= 0
            weight = jnp.where(live, weight_ref[pl.ds(line, 1), :], 0.0)
            local = jnp.where(live, cell - owner * CELL_DEV, -1).astype(jnp.float32)
            innovation = (values - obs_ref[pl.ds(line, 1), :]) * weight
            tail = whole * chunks + j * rest
            out_ref[step // 2, pl.ds(j * whole, whole), :] = innovation[:whole]
            out_ref[step // 2, pl.ds(tail, members - whole), :] = innovation[whole:]
            out_ref[step // 2, pl.ds(tail + members - whole, 1), :] = weight
            out_ref[step // 2, pl.ds(tail + members - whole + 1, 1), :] = local


def split(values):
    top = values.astype(jnp.bfloat16).astype(jnp.float32)
    return top, (values - top).astype(jnp.bfloat16).astype(jnp.float32)


def accumulate(members, chunks, in_refs, start_ref, acc_ref):
    rows, whole = block_rows(members)
    rest = rows - whole
    low_iota = lax.broadcasted_iota(jnp.int32, (WIDE, LANES), 0)
    low_half = low_iota.astype(jnp.float32).astype(jnp.bfloat16)
    one, nil = jnp.ones((), jnp.bfloat16), jnp.zeros((), jnp.bfloat16)
    row_iota = lax.broadcasted_iota(jnp.int32, (2 * rest, LANES), 0)
    blocks = [(ref, b) for ref, picks in in_refs for b in picks]
    for n, (ref, b) in enumerate(blocks):
        pieces, lows = [], []
        for j in range(chunks):
            tail = whole * chunks + j * rest
            main_top, main_rest = split(ref[b, pl.ds(j * whole, whole), :])
            end = ref[b, pl.ds(tail, rest), :]
            cell = end[members - whole + 1 : members - whole + 2].astype(jnp.int32)
            live = (cell >= 0).astype(jnp.float32)
            end = jnp.concatenate([end, end], 0)
            end = jnp.where(row_iota % rest == members - whole + 1, live, end)
            end_top, end_rest = split(end)
            end = jnp.where(row_iota < rest, end_top, end_rest)
            piece = jnp.concatenate([main_top, main_rest, end], 0)
            high = lax.shift_right_arithmetic(cell, 8)
            pieces.append([jnp.where(high == g, piece, 0.0) for g in range(GROUPS)])
            lows.append(jnp.where(low_half == (cell & (WIDE - 1)).astype(jnp.float32).astype(jnp.bfloat16), one, nil))
        left = jnp.concatenate(
            [jnp.concatenate([p[g] for p in pieces], 1) for g in range(GROUPS)], 0
        ).astype(jnp.bfloat16)
        low = jnp.concatenate(lows, 1)
        product = lax.dot_general(
            left, low, (((1,), (1,)), ((), ())), preferred_element_type=jnp.float32
        )
        if n:
            acc_ref[...] += product
        elif start_ref is None:
            acc_ref[...] = product
        else:
            acc_ref[...] = start_ref[...] + product


def finish(members, acc_ref, moment_ref, result_ref):
    rows, whole = block_rows(members)
    rest, extra = rows - whole, members - whole
    for g in range(GROUPS):
        start, width = g * WIDE, min(WIDE, CELL_DEV - g * WIDE)
        base = g * 2 * rows
        main = acc_ref[pl.ds(base, whole), :width] + acc_ref[pl.ds(base + whole, whole), :width]
        end = acc_ref[pl.ds(base + 2 * whole, 2 * rest), :width]
        end = end[:rest] + end[rest:]
        counted = end[extra + 1 : extra + 2]
        filled = counted > 0
        total = jnp.where(filled, end[extra : extra + 1], 1.0)
        inverse = 1.0 / total
        main = main * inverse
        last = end[:extra] * inverse
        moment = jnp.sum(main, 0, keepdims=True) + jnp.sum(last, 0, keepdims=True)
        mean = moment * (1.0 / members)
        main_gap, last_gap = main - mean, last - mean
        spread = jnp.sum(main_gap * main_gap, 0, keepdims=True) + jnp.sum(last_gap * last_gap, 0, keepdims=True)
        error = jnp.where(filled, inverse, 0.0)
        for j in range(width // LANES):
            line, cut = start // LANES + j, slice(j * LANES, (j + 1) * LANES)
            tail = LINES * whole + line * rest
            result_ref[line * whole : (line + 1) * whole, :] = main[:, cut]
            result_ref[tail : tail + extra, :] = last[:, cut]
            result_ref[tail + extra : tail + extra + 1, :] = error[:, cut]
            result_ref[tail + extra + 1 : tail + extra + 2, :] = counted[:, cut]
            moment_ref[0, line : line + 1, :] = moment[:, cut]
            moment_ref[1, line : line + 1, :] = spread[:, cut]


def near(array):
    return pltpu.with_memory_space_constraint(array, pltpu.VMEM)


def bin_some(members, chunks, arrays, start=None, last=False):
    acc = pltpu.VMEM((GROUPS * 2 * block_rows(members)[0], WIDE), jnp.float32)
    inputs = [array for array, _ in arrays] + ([] if start is None else [start])

    def body(*refs):
        ins, outs = refs[: len(inputs)], refs[len(inputs) :]
        start_ref = None if start is None else ins[-1]
        pairs = list(zip(ins, [picks for _, picks in arrays]))
        accumulate(members, chunks, pairs, start_ref, outs[-1])
        if last:
            finish(members, outs[-1], *outs[:-1])

    return pl.pallas_call(
        body,
        out_shape=[
            pltpu.VMEM((2, LINES, LANES), jnp.float32),
            pltpu.VMEM((LINES * block_rows(members)[0], LANES), jnp.float32),
        ]
        if last
        else acc,
        scratch_shapes=[acc] if last else [],
    )(*[near(array) for array in inputs])


def final_kernel(
    members, total, own_ref, passed_ref, moment_ref, out_ref, departure_ref, variance_ref, error_ref, count_ref
):
    mean = moment_ref[0] * (1.0 / total)
    departure_ref[...] = -mean
    variance_ref[...] = moment_ref[1] * (1.0 / (total - 1))

    rows, whole = block_rows(members)
    rest, extra = rows - whole, members - whole

    def write(result_ref):
        for j in range(LINES):
            cut = slice(j * LANES, (j + 1) * LANES)
            tail = LINES * whole + j * rest
            line, below = mean[j : j + 1], slice(tail + extra, tail + extra + 1)
            out_ref[:whole, cut] = result_ref[j * whole : (j + 1) * whole, :] - line
            out_ref[whole:, cut] = result_ref[tail : tail + extra, :] - line
            error_ref[j : j + 1, :] = result_ref[below, :]
            count_ref[j : j + 1, :] = result_ref[tail + extra + 1 : tail + extra + 2, :].astype(jnp.int32)

    odd = odd_plane()
    pl.when(odd == 0)(lambda: write(own_ref))
    pl.when(odd == 1)(lambda: write(passed_ref))


def merge(mine, theirs, each):
    gap = mine[0] - theirs[0]
    return jnp.stack([mine[0] + theirs[0], mine[1] + theirs[1] + gap * gap / (2 * each)])


def chip_order(chips):
    return list(range(chips - 1, 0, -1))


def step(member_values, obs_value, obs_weight, obs_cell):
    regions = lax.axis_size("reg")
    groups = lax.axis_size("mem")
    members, slots = member_values.shape
    chunks = slots // regions // LANES
    chips = regions // 2
    swap = [(i, i ^ 1) for i in range(regions)]
    lines = (slots // LANES, LANES)
    same, other = pl.pallas_call(
        functools.partial(pack_kernel, members, regions, chunks),
        out_shape=[pltpu.VMEM((chips, chunks * block_rows(members)[0], LANES), jnp.float32)] * 2,
    )(member_values, obs_value.reshape(lines), obs_weight.reshape(lines), obs_cell.reshape(lines))
    partner = lax.ppermute(other, "reg", swap)
    arrivals = []
    for k in chip_order(chips):
        sent = jnp.stack([same[k], partner[k]])
        pairs = [(i, i ^ (2 * k + 1)) for i in range(regions)]
        arrivals.append((lax.ppermute(sent, "reg", pairs), (0, 1)))
    sums = bin_some(members, chunks, [(same, (0,)), (partner, (0,))])
    for n, arrival in enumerate(arrivals):
        sums = bin_some(members, chunks, [arrival], sums, n == chips - 2)
    moments, own = sums
    passed = lax.ppermute(own, "reg", swap)
    each, reach = members, 1
    while reach < groups:
        pairs = [(z * regions + i, (z ^ reach) * regions + (i ^ 1)) for z in range(groups) for i in range(regions)]
        theirs = lax.ppermute(moments, ("mem", "reg"), pairs)
        moments = merge(moments, theirs, each)
        each, reach = 2 * each, 2 * reach
    moments = lax.cond(odd_plane() == 1, lambda m: lax.ppermute(m, "reg", swap), lambda m: m, moments)
    cells = jax.ShapeDtypeStruct((LINES, LANES), jnp.float32)
    outs = pl.pallas_call(
        functools.partial(final_kernel, members, members * groups),
        out_shape=[
            jax.ShapeDtypeStruct((members, CELL_DEV), jnp.float32),
            cells,
            cells,
            cells,
            jax.ShapeDtypeStruct((LINES, LANES), jnp.int32),
        ],
    )(*[near(a) for a in (own, passed, moments)])
    return (outs[0], *[out.reshape(-1) for out in outs[1:]])


def solution(mesh):
    return jax.shard_map(
        step,
        mesh=mesh,
        in_specs=(P("mem", "reg"), P("reg"), P("reg"), P("reg")),
        out_specs=(P("mem", "reg"), P("reg"), P("reg"), P("reg"), P("reg")),
        check_vma=False,
    )
```

time: 21.2 us -> 20.5 us (0.967)
  the two profiles are of different devices: /device:TPU:0 before, /device:TPU:19 now
where the time goes in v4:
time: 20.5 us; the launch traced here: 20.4 us
  waiting for transfers between devices  11 us (54%)
  starting transfers between devices  5.43 us (26%)
  Pallas kernels  3.19 us (16%)
  between operations  0.71 us (3%)
    ppermute x2, waiting for transfers between devices, step(): theirs = lax.ppermute(moments, ('mem', 'reg'), pairs)  5.97 us
    ppermute x3, starting transfers between devices, step(): arrivals.append((lax.ppermute(sent, 'reg', pairs), (0, 1)))  3.24 us
    ppermute x3, waiting for transfers between devices, step(): arrivals.append((lax.ppermute(sent, 'reg', pairs), (0, 1)))  2.89 us
    pallas_call x4, Pallas kernels, bin_some(): pl.pallas_call(body, out_shape=[pltpu.VMEM((2, LINES, LANES), jnp.float32...  1.44 us
    ppermute x1, waiting for transfers between devices, step(): lax.ppermute(m, 'reg', swap)  1.17 us
    pallas_call x1, Pallas kernels, step(): pl.pallas_call(functools.partial(pack_kernel, members, regions, chunks),...  1.05 us
    ppermute x2, starting transfers between devices, step(): theirs = lax.ppermute(moments, ('mem', 'reg'), pairs)  0.95 us
    ppermute x1, waiting for transfers between devices, step(): partner = lax.ppermute(other, 'reg', swap)  0.94 us
  transfers between devices with their start and end apart: 8, of which 5 were waited for; matrix products, arithmetic and copies ran while one was open for 0% of the time, Pallas kernels for 5%

profile of v4, /device:TPU:19, one launch (start us, length us, event | category | flops | bytes accessed | tf_op | source)
XLA Modules:
  0.0 20.4 jit_solution(4613792590558760268)
XLA Ops:
  0.6 1.1 %shard_map.83 = (f32[4,48,128]{2,1,0:T(8,128)S(1)}, f32[4,48,128]{2,1,0:T(8,128)S(1)}) custom-call(f32[10,4096]{1,0:T(8,128)} %value_ref.1, f32[32,128]{1,0:T(8,128)} %bitcast.7, f32[32,128]{1,0:T(8,128)} %bitcast.8, s32[32,128]{1,0:T(8,128)} %bitcast.9), custom_call_target="tpu_custom_call" | custom-call | tf_op jit(solution)/shard_map/pallas_call | solution.py:200
  1.7 0.7 %collective-permute-start.1 = (f32[4,48,128]{2,1,0:T(8,128)S(1)}, f32[4,48,128]{2,1,0:T(8,128)S(1)}, u32[]{:S(2)}, u32[]{:S(2)}) collective-permute-start(f32[4,48,128]{2,1,0:T(8,128)S(1)} %get-tuple-element.20), channel_id=1, source_target_pairs={{0,1},{1,0},{2,3},{3,2},{4,5},{5,4},{6,7},{7,6},{8,9},{9,8},{10,11... | collective-permute-start | bytes 294920 | tf_op jit(solution)/shard_map/ppermute | solution.py:204
  2.4 0.9 %collective-permute-done.1.refs_1_ = f32[4,48,128]{2,1,0:T(8,128)S(1)} collective-permute-done((f32[4,48,128]{2,1,0:T(8,128)S(1)}, f32[4,48,128]{2,1,0:T(8,128)S(1)}, u32[]{:S(2)}, u32[]{:S(2)}) %collective-permute-start.1) | collective-permute-done | bytes 98336 | tf_op jit(solution)/shard_map/ppermute | solution.py:204
  3.4 1.5 %collective-permute-start.3 = (f32[2,48,128]{2,1,0:T(8,128)S(1)}, f32[2,48,128]{2,1,0:T(8,128)S(1)}, u32[]{:S(2)}, u32[]{:S(2)}) collective-permute-start(f32[2,48,128]{2,1,0:T(8,128)S(1)} %pad_maximum_fusion.1), channel_id=1, source_target_pairs={{0,5},{1,4},{2,7},{3,6},{4,1},{5,0},{6,3},{7,2},{8,13},{9,12},{10,... | collective-permute-start | bytes 147464 | tf_op jit(solution)/shard_map/ppermute | solution.py:209
  4.9 0.2 %collective-permute-start.4 = (f32[2,48,128]{2,1,0:T(8,128)S(1)}, f32[2,48,128]{2,1,0:T(8,128)S(1)}, u32[]{:S(2)}, u32[]{:S(2)}) collective-permute-start(f32[2,48,128]{2,1,0:T(8,128)S(1)} %pad_maximum_fusion.2), channel_id=1, source_target_pairs={{0,7},{1,6},{2,5},{3,4},{4,3},{5,2},{6,1},{7,0},{8,15},{9,14},{10,... | collective-permute-start | bytes 147464 | tf_op jit(solution)/shard_map/ppermute | solution.py:209
  5.2 1.5 %collective-permute-start.2 = (f32[2,48,128]{2,1,0:T(8,128)S(1)}, f32[2,48,128]{2,1,0:T(8,128)S(1)}, u32[]{:S(2)}, u32[]{:S(2)}) collective-permute-start(f32[2,48,128]{2,1,0:T(8,128)S(1)} %pad_maximum_fusion), channel_id=1, source_target_pairs={{0,3},{1,2},{2,1},{3,0},{4,7},{5,6},{6,5},{7,4},{8,11},{9,10},{10,... | collective-permute-start | bytes 147464 | tf_op jit(solution)/shard_map/ppermute | solution.py:209
  6.6 0.3 %shard_map.84.refs_1_ = f32[192,256]{1,0:T(8,128)S(1)} custom-call(f32[4,48,128]{2,1,0:T(8,128)S(1)} %get-tuple-element.19.refs_0_, f32[4,48,128]{2,1,0:T(8,128)S(1)} %collective-permute-done.1.refs_1_), custom_call_target="tpu_custom_call" | custom-call | tf_op jit(solution)/shard_map/pallas_call | solution.py:146
  7.0 2.9 %collective-permute-done.4.refs_0_ = f32[2,48,128]{2,1,0:T(8,128)S(1)} collective-permute-done((f32[2,48,128]{2,1,0:T(8,128)S(1)}, f32[2,48,128]{2,1,0:T(8,128)S(1)}, u32[]{:S(2)}, u32[]{:S(2)}) %collective-permute-start.4) | collective-permute-done | bytes 49184 | tf_op jit(solution)/shard_map/ppermute | solution.py:209
  9.9 0.3 %shard_map.85.refs_1_ = f32[192,256]{1,0:T(8,128)S(1)} custom-call(f32[2,48,128]{2,1,0:T(8,128)S(1)} %collective-permute-done.4.refs_0_, f32[192,256]{1,0:T(8,128)S(1)} %shard_map.84.refs_1_), custom_call_target="tpu_custom_call" | custom-call | tf_op jit(solution)/shard_map/pallas_call | solution.py:146
  10.2 0.0 collective-permute-done.3.refs_0_
  10.2 0.3 %shard_map.86.refs_1_ = f32[192,256]{1,0:T(8,128)S(1)} custom-call(f32[2,48,128]{2,1,0:T(8,128)S(1)} %collective-permute-done.3.refs_0_, f32[192,256]{1,0:T(8,128)S(1)} %shard_map.85.refs_1_), custom_call_target="tpu_custom_call" | custom-call | tf_op jit(solution)/shard_map/pallas_call | solution.py:146
  10.6 0.0 collective-permute-done.2.refs_0_
  10.6 0.4 %shard_map.87 = (f32[2,15,128]{2,1,0:T(8,128)S(1)}, f32[180,128]{1,0:T(8,128)S(1)}) custom-call(f32[2,48,128]{2,1,0:T(8,128)S(1)} %collective-permute-done.2.refs_0_, f32[192,256]{1,0:T(8,128)S(1)} %shard_map.86.refs_1_), custom_call_target="tpu_custom_call" | custom-call | tf_op jit(solution)/shard_map/pallas_call | solution.py:146
  11.0 0.9 %collective-permute-start.6 = (f32[2,15,128]{2,1,0:T(8,128)S(1)}, f32[2,15,128]{2,1,0:T(8,128)S(1)}, u32[]{:S(2)}, u32[]{:S(2)}) collective-permute-start(f32[2,15,128]{2,1,0:T(8,128)S(1)} %get-tuple-element.22), channel_id=1, source_target_pairs={{0,9},{1,8},{2,11},{3,10},{4,13},{5,12},{6,15},{7,14},{8,1},{9,0},... | collective-permute-start | bytes 46088 | tf_op jit(solution)/shard_map/ppermute | solution.py:218
  11.9 2.3 %collective-permute-done.6 = f32[2,15,128]{2,1,0:T(8,128)S(1)} collective-permute-done((f32[2,15,128]{2,1,0:T(8,128)S(1)}, f32[2,15,128]{2,1,0:T(8,128)S(1)}, u32[]{:S(2)}, u32[]{:S(2)}) %collective-permute-start.6) | collective-permute-done | bytes 15392 | tf_op jit(solution)/shard_map/ppermute | solution.py:218
  14.3 0.1 collective-permute-start.7
  14.3 0.4 %collective-permute-start.5 = (f32[180,128]{1,0:T(8,128)S(1)}, f32[180,128]{1,0:T(8,128)S(1)}, u32[]{:S(2)}, u32[]{:S(2)}) collective-permute-start(f32[180,128]{1,0:T(8,128)S(1)} %get-tuple-element.21.own_ref), channel_id=1, source_target_pairs={{0,1},{1,0},{2,3},{3,2},{4,5},{5,4},{6,7},{7,6},{8,9},{9,8},{10,11... | collective-permute-start | bytes 276488 | tf_op jit(solution)/shard_map/ppermute | solution.py:214
  14.8 3.6 %collective-permute-done.7 = f32[2,15,128]{2,1,0:T(8,128)S(1)} collective-permute-done((f32[2,15,128]{2,1,0:T(8,128)S(1)}, f32[2,15,128]{2,1,0:T(8,128)S(1)}, u32[]{:S(2)}, u32[]{:S(2)}) %collective-permute-start.7) | collective-permute-done | bytes 15392 | tf_op jit(solution)/shard_map/ppermute | solution.py:218
  18.4 1.3 %conditional.1 = (f32[2,15,128]{2,1,0:T(8,128)S(1)}) conditional(s32[]{:T(128)} %convert_element_type.3, f32[2,15,128]{2,1,0:T(8,128)S(1)} %pad_maximum_fusion.4, f32[2,15,128]{2,1,0:T(8,128)S(1)} %pad_maximum_fusion.4), branch_computations={%region_0.0_spmd, %region_1.0_spmd} | conditional | bytes 92208 | solution.py:221
  18.4 0.1 collective-permute-start
  18.5 1.2 %collective-permute-done = f32[2,15,128]{2,1,0:T(8,128)S(1)} collective-permute-done((f32[2,15,128]{2,1,0:T(8,128)S(1)}, f32[2,15,128]{2,1,0:T(8,128)S(1)}, u32[]{:S(2)}, u32[]{:S(2)}) %collective-permute-start) | collective-permute-done | bytes 15392 | tf_op jit(solution)/shard_map/cond/branch_1_fun/ppermute | solution.py:221
  19.7 0.0 collective-permute-done.5.passed_ref
  19.7 0.7 %shard_map.88 = (f32[10,1920]{1,0:T(8,128)}, f32[15,128]{1,0:T(8,128)}, f32[15,128]{1,0:T(8,128)}, f32[15,128]{1,0:T(8,128)}, s32[15,128]{1,0:T(8,128)}) custom-call(f32[180,128]{1,0:T(8,128)S(1)} %get-tuple-element.21.own_ref, f32[180,128]{1,0:T(8,128)S(1)} %collective-permute-done.5.passed_ref, f32[2,15,128]{2,1,0:T(8,128)S(1)} %get-tuple-element.38.moment_ref), custom_call_target="tpu_custom_call" | custom-call | tf_op jit(solution)/shard_map/pallas_call | solution.py:223
  (10 shorter events, 0.1 us)
Async XLA Ops:
  1.7 1.7 %collective-permute-start.1 = (f32[4,48,128]{2,1,0:T(8,128)S(1)}, f32[4,48,128]{2,1,0:T(8,128)S(1)}, u32[]{:S(2)}, u32[]{:S(2)}) collective-permute-start(f32[4,48,128]{2,1,0:T(8,128)S(1)} %get-tuple-element.20), channel_id=1, source_target_pairs={{0,1},{1,0},{2,3},{3,2},{4,5},{5,4},{6,7},{7,6},{8,9},{9,8},{10,11... | collective-permute-start | bytes 294920 | tf_op jit(solution)/shard_map/ppermute | solution.py:204
  3.4 6.8 %collective-permute-start.3 = (f32[2,48,128]{2,1,0:T(8,128)S(1)}, f32[2,48,128]{2,1,0:T(8,128)S(1)}, u32[]{:S(2)}, u32[]{:S(2)}) collective-permute-start(f32[2,48,128]{2,1,0:T(8,128)S(1)} %pad_maximum_fusion.1), channel_id=1, source_target_pairs={{0,5},{1,4},{2,7},{3,6},{4,1},{5,0},{6,3},{7,2},{8,13},{9,12},{10,... | collective-permute-start | bytes 147464 | tf_op jit(solution)/shard_map/ppermute | solution.py:209
  4.9 4.9 %collective-permute-start.4 = (f32[2,48,128]{2,1,0:T(8,128)S(1)}, f32[2,48,128]{2,1,0:T(8,128)S(1)}, u32[]{:S(2)}, u32[]{:S(2)}) collective-permute-start(f32[2,48,128]{2,1,0:T(8,128)S(1)} %pad_maximum_fusion.2), channel_id=1, source_target_pairs={{0,7},{1,6},{2,5},{3,4},{4,3},{5,2},{6,1},{7,0},{8,15},{9,14},{10,... | collective-permute-start | bytes 147464 | tf_op jit(solution)/shard_map/ppermute | solution.py:209
  5.2 5.4 %collective-permute-start.2 = (f32[2,48,128]{2,1,0:T(8,128)S(1)}, f32[2,48,128]{2,1,0:T(8,128)S(1)}, u32[]{:S(2)}, u32[]{:S(2)}) collective-permute-start(f32[2,48,128]{2,1,0:T(8,128)S(1)} %pad_maximum_fusion), channel_id=1, source_target_pairs={{0,3},{1,2},{2,1},{3,0},{4,7},{5,6},{6,5},{7,4},{8,11},{9,10},{10,... | collective-permute-start | bytes 147464 | tf_op jit(solution)/shard_map/ppermute | solution.py:209
  11.0 3.2 %collective-permute-start.6 = (f32[2,15,128]{2,1,0:T(8,128)S(1)}, f32[2,15,128]{2,1,0:T(8,128)S(1)}, u32[]{:S(2)}, u32[]{:S(2)}) collective-permute-start(f32[2,15,128]{2,1,0:T(8,128)S(1)} %get-tuple-element.22), channel_id=1, source_target_pairs={{0,9},{1,8},{2,11},{3,10},{4,13},{5,12},{6,15},{7,14},{8,1},{9,0},... | collective-permute-start | bytes 46088 | tf_op jit(solution)/shard_map/ppermute | solution.py:218
  14.3 4.1 %collective-permute-start.7 = (f32[2,15,128]{2,1,0:T(8,128)S(1)}, f32[2,15,128]{2,1,0:T(8,128)S(1)}, u32[]{:S(2)}, u32[]{:S(2)}) collective-permute-start(f32[2,15,128]{2,1,0:T(8,128)S(1)} %pad_maximum_fusion.3), channel_id=1, source_target_pairs={{0,17},{1,16},{2,19},{3,18},{4,21},{5,20},{6,23},{7,22},{8,25},{9,... | collective-permute-start | bytes 46088 | tf_op jit(solution)/shard_map/ppermute | solution.py:218
  14.3 5.3 %collective-permute-start.5 = (f32[180,128]{1,0:T(8,128)S(1)}, f32[180,128]{1,0:T(8,128)S(1)}, u32[]{:S(2)}, u32[]{:S(2)}) collective-permute-start(f32[180,128]{1,0:T(8,128)S(1)} %get-tuple-element.21.own_ref), channel_id=1, source_target_pairs={{0,1},{1,0},{2,3},{3,2},{4,5},{5,4},{6,7},{7,6},{8,9},{9,8},{10,11... | collective-permute-start | bytes 276488 | tf_op jit(solution)/shard_map/ppermute | solution.py:214
  18.4 1.2 %collective-permute-start = (f32[2,15,128]{2,1,0:T(8,128)S(1)}, f32[2,15,128]{2,1,0:T(8,128)S(1)}, u32[]{:S(2)}, u32[]{:S(2)}) collective-permute-start(f32[2,15,128]{2,1,0:T(8,128)S(1)} %param.1), channel_id=1, source_target_pairs={{0,1},{1,0},{2,3},{3,2},{4,5},{5,4},{6,7},{7,6},{8,9},{9,8},{10,11... | collective-permute-start | bytes 46088 | tf_op jit(solution)/shard_map/cond/branch_1_fun/ppermute | solution.py:221

commit v5 on v4

--- a/solution.py
+++ b/solution.py
@@ -30,13 +30,16 @@
     return odd
 
 
-def pack_kernel(members, regions, chunks, value_ref, obs_ref, weight_ref, cell_ref, same_ref, other_ref):
+def pack_kernel(members, regions, chunks, value_ref, obs_ref, weight_ref, cell_ref, same_ref, other_ref, direct_ref):
     me, odd = lax.axis_index("reg"), odd_plane()
     rows, whole = block_rows(members)
     rest = rows - whole
     for step in range(regions):
         owner = me ^ step ^ odd
-        out_ref = other_ref if (step % 2) ^ (step > 1) else same_ref
+        if step // 2 == regions // 2 - 1:
+            out_ref, slot = direct_ref, 1 - step % 2
+        else:
+            out_ref, slot = other_ref if (step % 2) ^ (step > 1) else same_ref, step // 2
         for j in range(chunks):
             line = owner * chunks + j
             values = value_ref[:, pl.ds(pl.multiple_of(line * LANES, LANES), LANES)]
@@ -46,10 +49,10 @@
             local = jnp.where(live, cell - owner * CELL_DEV, -1).astype(jnp.float32)
             innovation = (values - obs_ref[pl.ds(line, 1), :]) * weight
             tail = whole * chunks + j * rest
-            out_ref[step // 2, pl.ds(j * whole, whole), :] = innovation[:whole]
-            out_ref[step // 2, pl.ds(tail, members - whole), :] = innovation[whole:]
-            out_ref[step // 2, pl.ds(tail + members - whole, 1), :] = weight
-            out_ref[step // 2, pl.ds(tail + members - whole + 1, 1), :] = local
+            out_ref[slot, pl.ds(j * whole, whole), :] = innovation[:whole]
+            out_ref[slot, pl.ds(tail, members - whole), :] = innovation[whole:]
+            out_ref[slot, pl.ds(tail + members - whole, 1), :] = weight
+            out_ref[slot, pl.ds(tail + members - whole + 1, 1), :] = local
 
 
 def split(values):
@@ -197,19 +200,23 @@
     chips = regions // 2
     swap = [(i, i ^ 1) for i in range(regions)]
     lines = (slots // LANES, LANES)
-    same, other = pl.pallas_call(
+    shape = (chunks * block_rows(members)[0], LANES)
+    same, other, direct = pl.pallas_call(
         functools.partial(pack_kernel, members, regions, chunks),
-        out_shape=[pltpu.VMEM((chips, chunks * block_rows(members)[0], LANES), jnp.float32)] * 2,
+        out_shape=[pltpu.VMEM((n, *shape), jnp.float32) for n in (chips - 1, chips - 1, 2)],
     )(member_values, obs_value.reshape(lines), obs_weight.reshape(lines), obs_cell.reshape(lines))
     partner = lax.ppermute(other, "reg", swap)
     arrivals = []
     for k in chip_order(chips):
-        sent = jnp.stack([same[k], partner[k]])
+        sent = direct if k == chips - 1 else jnp.stack([same[k], partner[k]])
         pairs = [(i, i ^ (2 * k + 1)) for i in range(regions)]
         arrivals.append((lax.ppermute(sent, "reg", pairs), (0, 1)))
+    landed = arrivals[0][0]
+    forwarded = (lax.ppermute(landed, "reg", swap), (1,))
     sums = bin_some(members, chunks, [(same, (0,)), (partner, (0,))])
     for n, arrival in enumerate(arrivals):
-        sums = bin_some(members, chunks, [arrival], sums, n == chips - 2)
+        taken = [(landed, (0,))] if n == 0 else [arrival, forwarded] if n == 2 else [arrival]
+        sums = bin_some(members, chunks, taken, sums, n == chips - 2)
     moments, own = sums
     passed = lax.ppermute(own, "reg", swap)
     each, reach = members, 1

time: 20.5 us -> 22.1 us (1.078)
  the two profiles are of different devices: /device:TPU:19 before, /device:TPU:17 now
where the time goes in v5:
time: 22.1 us; the launch traced here: 21.9 us
  waiting for transfers between devices  10.3 us (47%)
  starting transfers between devices  7.72 us (35%)
  Pallas kernels  3.19 us (14%)
  between operations  0.7 us (3%)
    ppermute x2, waiting for transfers between devices, step(): theirs = lax.ppermute(moments, ('mem', 'reg'), pairs)  5.52 us
    ppermute x3, starting transfers between devices, step(): arrivals.append((lax.ppermute(sent, 'reg', pairs), (0, 1)))  4.93 us
    ppermute x3, waiting for transfers between devices, step(): arrivals.append((lax.ppermute(sent, 'reg', pairs), (0, 1)))  3.64 us
    pallas_call x4, Pallas kernels, bin_some(): pl.pallas_call(body, out_shape=[pltpu.VMEM((2, LINES, LANES), jnp.float32...  1.45 us
    ppermute x2, starting transfers between devices, step(): theirs = lax.ppermute(moments, ('mem', 'reg'), pairs)  1.4 us
    ppermute x1, waiting for transfers between devices, step(): lax.ppermute(m, 'reg', swap)  1.1 us
    pallas_call x1, Pallas kernels, step(): pl.pallas_call(functools.partial(pack_kernel, members, regions, chunks),...  1.05 us
    ppermute x1, starting transfers between devices, step(): partner = lax.ppermute(other, 'reg', swap)  0.74 us
  transfers between devices with their start and end apart: 9, of which 6 were waited for; matrix products, arithmetic and copies ran while one was open for 0% of the time, Pallas kernels for 4%

profile of v5, /device:TPU:17, one launch (start us, length us, event | category | flops | bytes accessed | tf_op | source)
XLA Modules:
  0.0 21.9 jit_solution(9463839298808522764)
XLA Ops:
  0.6 1.1 %shard_map.83 = (f32[3,48,128]{2,1,0:T(8,128)S(1)}, f32[3,48,128]{2,1,0:T(8,128)S(1)}, f32[2,48,128]{2,1,0:T(8,128)S(1)}) custom-call(f32[10,4096]{1,0:T(8,128)} %value_ref.1, f32[32,128]{1,0:T(8,128)} %bitcast.7, f32[32,128]{1,0:T(8,128)} %bitcast.8, s32[32,128]{1,0:T(8,128)} %bitcast.9), custom_call_target="tpu_custom_call" | custom-call | tf_op jit(solution)/shard_map/pallas_call | solution.py:204
  1.7 0.7 %collective-permute-start.1 = (f32[3,48,128]{2,1,0:T(8,128)S(1)}, f32[3,48,128]{2,1,0:T(8,128)S(1)}, u32[]{:S(2)}, u32[]{:S(2)}) collective-permute-start(f32[3,48,128]{2,1,0:T(8,128)S(1)} %get-tuple-element.21), channel_id=1, source_target_pairs={{0,1},{1,0},{2,3},{3,2},{4,5},{5,4},{6,7},{7,6},{8,9},{9,8},{10,11... | collective-permute-start | bytes 221192 | tf_op jit(solution)/shard_map/ppermute | solution.py:208
  2.4 2.1 %collective-permute-start.3 = (f32[2,48,128]{2,1,0:T(8,128)S(1)}, f32[2,48,128]{2,1,0:T(8,128)S(1)}, u32[]{:S(2)}, u32[]{:S(2)}) collective-permute-start(f32[2,48,128]{2,1,0:T(8,128)S(1)} %get-tuple-element.22), channel_id=1, source_target_pairs={{0,7},{1,6},{2,5},{3,4},{4,3},{5,2},{6,1},{7,0},{8,15},{9,14},{10,... | collective-permute-start | bytes 147464 | tf_op jit(solution)/shard_map/ppermute | solution.py:213
  4.6 2.3 %collective-permute-done.3.refs_0_ = f32[2,48,128]{2,1,0:T(8,128)S(1)} collective-permute-done((f32[2,48,128]{2,1,0:T(8,128)S(1)}, f32[2,48,128]{2,1,0:T(8,128)S(1)}, u32[]{:S(2)}, u32[]{:S(2)}) %collective-permute-start.3) | collective-permute-done | bytes 49184 | tf_op jit(solution)/shard_map/ppermute | solution.py:213
  6.8 0.1 collective-permute-start.4
  6.9 0.0 collective-permute-done.1.refs_1_
  6.9 1.6 %collective-permute-start.5 = (f32[2,48,128]{2,1,0:T(8,128)S(1)}, f32[2,48,128]{2,1,0:T(8,128)S(1)}, u32[]{:S(2)}, u32[]{:S(2)}) collective-permute-start(f32[2,48,128]{2,1,0:T(8,128)S(1)} %pad_maximum_fusion.1), channel_id=1, source_target_pairs={{0,5},{1,4},{2,7},{3,6},{4,1},{5,0},{6,3},{7,2},{8,13},{9,12},{10,... | collective-permute-start | bytes 147464 | tf_op jit(solution)/shard_map/ppermute | solution.py:213
  8.6 1.2 %collective-permute-start.2 = (f32[2,48,128]{2,1,0:T(8,128)S(1)}, f32[2,48,128]{2,1,0:T(8,128)S(1)}, u32[]{:S(2)}, u32[]{:S(2)}) collective-permute-start(f32[2,48,128]{2,1,0:T(8,128)S(1)} %pad_maximum_fusion), channel_id=1, source_target_pairs={{0,3},{1,2},{2,1},{3,0},{4,7},{5,6},{6,5},{7,4},{8,11},{9,10},{10,... | collective-permute-start | bytes 147464 | tf_op jit(solution)/shard_map/ppermute | solution.py:213
  9.7 0.3 %shard_map.84.refs_1_ = f32[192,256]{1,0:T(8,128)S(1)} custom-call(f32[3,48,128]{2,1,0:T(8,128)S(1)} %get-tuple-element.20.refs_0_, f32[3,48,128]{2,1,0:T(8,128)S(1)} %collective-permute-done.1.refs_1_), custom_call_target="tpu_custom_call" | custom-call | tf_op jit(solution)/shard_map/pallas_call | solution.py:149
  10.1 0.3 %shard_map.85.refs_1_ = f32[192,256]{1,0:T(8,128)S(1)} custom-call(f32[2,48,128]{2,1,0:T(8,128)S(1)} %collective-permute-done.3.refs_0_, f32[192,256]{1,0:T(8,128)S(1)} %shard_map.84.refs_1_), custom_call_target="tpu_custom_call" | custom-call | tf_op jit(solution)/shard_map/pallas_call | solution.py:149
  10.4 0.5 %collective-permute-done.5.refs_0_ = f32[2,48,128]{2,1,0:T(8,128)S(1)} collective-permute-done((f32[2,48,128]{2,1,0:T(8,128)S(1)}, f32[2,48,128]{2,1,0:T(8,128)S(1)}, u32[]{:S(2)}, u32[]{:S(2)}) %collective-permute-start.5) | collective-permute-done | bytes 49184 | tf_op jit(solution)/shard_map/ppermute | solution.py:213
  10.8 0.3 %shard_map.86.refs_2_ = f32[192,256]{1,0:T(8,128)S(1)} custom-call(f32[2,48,128]{2,1,0:T(8,128)S(1)} %collective-permute-done.5.refs_0_, f32[192,256]{1,0:T(8,128)S(1)} %shard_map.85.refs_1_), custom_call_target="tpu_custom_call" | custom-call | tf_op jit(solution)/shard_map/pallas_call | solution.py:149
  11.2 0.0 collective-permute-done.4.refs_1_
  11.2 0.9 %collective-permute-done.2.refs_0_ = f32[2,48,128]{2,1,0:T(8,128)S(1)} collective-permute-done((f32[2,48,128]{2,1,0:T(8,128)S(1)}, f32[2,48,128]{2,1,0:T(8,128)S(1)}, u32[]{:S(2)}, u32[]{:S(2)}) %collective-permute-start.2) | collective-permute-done | bytes 49184 | tf_op jit(solution)/shard_map/ppermute | solution.py:213
  12.1 0.5 %shard_map.87 = (f32[2,15,128]{2,1,0:T(8,128)S(1)}, f32[180,128]{1,0:T(8,128)S(1)}) custom-call(f32[2,48,128]{2,1,0:T(8,128)S(1)} %collective-permute-done.2.refs_0_, f32[2,48,128]{2,1,0:T(8,128)S(1)} %collective-permute-done.4.refs_1_, f32[192,256]{1,0:T(8,128)S(1)} %shard_map.86.refs_2_), custom_call_target="tpu_custom_call" | custom-call | tf_op jit(solution)/shard_map/pallas_call | solution.py:149
  12.6 1.3 %collective-permute-start.7 = (f32[2,15,128]{2,1,0:T(8,128)S(1)}, f32[2,15,128]{2,1,0:T(8,128)S(1)}, u32[]{:S(2)}, u32[]{:S(2)}) collective-permute-start(f32[2,15,128]{2,1,0:T(8,128)S(1)} %get-tuple-element.24), channel_id=1, source_target_pairs={{0,9},{1,8},{2,11},{3,10},{4,13},{5,12},{6,15},{7,14},{8,1},{9,0},... | collective-permute-start | bytes 46088 | tf_op jit(solution)/shard_map/ppermute | solution.py:225
  13.9 1.9 %collective-permute-done.7 = f32[2,15,128]{2,1,0:T(8,128)S(1)} collective-permute-done((f32[2,15,128]{2,1,0:T(8,128)S(1)}, f32[2,15,128]{2,1,0:T(8,128)S(1)}, u32[]{:S(2)}, u32[]{:S(2)}) %collective-permute-start.7) | collective-permute-done | bytes 15392 | tf_op jit(solution)/shard_map/ppermute | solution.py:225
  15.8 0.1 collective-permute-start.8
  15.9 0.4 %collective-permute-start.6 = (f32[180,128]{1,0:T(8,128)S(1)}, f32[180,128]{1,0:T(8,128)S(1)}, u32[]{:S(2)}, u32[]{:S(2)}) collective-permute-start(f32[180,128]{1,0:T(8,128)S(1)} %get-tuple-element.23.own_ref), channel_id=1, source_target_pairs={{0,1},{1,0},{2,3},{3,2},{4,5},{5,4},{6,7},{7,6},{8,9},{9,8},{10,11... | collective-permute-start | bytes 276488 | tf_op jit(solution)/shard_map/ppermute | solution.py:221
  16.4 3.6 %collective-permute-done.8 = f32[2,15,128]{2,1,0:T(8,128)S(1)} collective-permute-done((f32[2,15,128]{2,1,0:T(8,128)S(1)}, f32[2,15,128]{2,1,0:T(8,128)S(1)}, u32[]{:S(2)}, u32[]{:S(2)}) %collective-permute-start.8) | collective-permute-done | bytes 15392 | tf_op jit(solution)/shard_map/ppermute | solution.py:225
  20.0 1.3 %conditional.1 = (f32[2,15,128]{2,1,0:T(8,128)S(1)}) conditional(s32[]{:T(128)} %convert_element_type.3, f32[2,15,128]{2,1,0:T(8,128)S(1)} %pad_maximum_fusion.3, f32[2,15,128]{2,1,0:T(8,128)S(1)} %pad_maximum_fusion.3), branch_computations={%region_0.0_spmd, %region_1.0_spmd} | conditional | bytes 92208 | solution.py:228
  20.0 0.1 collective-permute-start
  20.1 1.1 %collective-permute-done = f32[2,15,128]{2,1,0:T(8,128)S(1)} collective-permute-done((f32[2,15,128]{2,1,0:T(8,128)S(1)}, f32[2,15,128]{2,1,0:T(8,128)S(1)}, u32[]{:S(2)}, u32[]{:S(2)}) %collective-permute-start) | collective-permute-done | bytes 15392 | tf_op jit(solution)/shard_map/cond/branch_1_fun/ppermute | solution.py:228
  21.2 0.0 collective-permute-done.6.passed_ref
  21.3 0.7 %shard_map.88 = (f32[10,1920]{1,0:T(8,128)}, f32[15,128]{1,0:T(8,128)}, f32[15,128]{1,0:T(8,128)}, f32[15,128]{1,0:T(8,128)}, s32[15,128]{1,0:T(8,128)}) custom-call(f32[180,128]{1,0:T(8,128)S(1)} %get-tuple-element.23.own_ref, f32[180,128]{1,0:T(8,128)S(1)} %collective-permute-done.6.passed_ref, f32[2,15,128]{2,1,0:T(8,128)S(1)} %get-tuple-element.38.moment_ref), custom_call_target="tpu_custom_call" | custom-call | tf_op jit(solution)/shard_map/pallas_call | solution.py:230
  (9 shorter events, 0.0 us)
Async XLA Ops:
  1.7 5.2 %collective-permute-start.1 = (f32[3,48,128]{2,1,0:T(8,128)S(1)}, f32[3,48,128]{2,1,0:T(8,128)S(1)}, u32[]{:S(2)}, u32[]{:S(2)}) collective-permute-start(f32[3,48,128]{2,1,0:T(8,128)S(1)} %get-tuple-element.21), channel_id=1, source_target_pairs={{0,1},{1,0},{2,3},{3,2},{4,5},{5,4},{6,7},{7,6},{8,9},{9,8},{10,11... | collective-permute-start | bytes 221192 | tf_op jit(solution)/shard_map/ppermute | solution.py:208
  2.4 4.4 %collective-permute-start.3 = (f32[2,48,128]{2,1,0:T(8,128)S(1)}, f32[2,48,128]{2,1,0:T(8,128)S(1)}, u32[]{:S(2)}, u32[]{:S(2)}) collective-permute-start(f32[2,48,128]{2,1,0:T(8,128)S(1)} %get-tuple-element.22), channel_id=1, source_target_pairs={{0,7},{1,6},{2,5},{3,4},{4,3},{5,2},{6,1},{7,0},{8,15},{9,14},{10,... | collective-permute-start | bytes 147464 | tf_op jit(solution)/shard_map/ppermute | solution.py:213
  6.8 4.3 %collective-permute-start.4 = (f32[2,48,128]{2,1,0:T(8,128)S(1)}, f32[2,48,128]{2,1,0:T(8,128)S(1)}, u32[]{:S(2)}, u32[]{:S(2)}) collective-permute-start(f32[2,48,128]{2,1,0:T(8,128)S(1)} %collective-permute-done.3.refs_0_), channel_id=1, source_target_pairs={{0,1},{1,0},{2,3},{3,2},{4,5},{5,4},{6,7},{7,6},{8,9},{9,8},{10,11... | collective-permute-start | bytes 147464 | tf_op jit(solution)/shard_map/ppermute | solution.py:215
  6.9 3.9 %collective-permute-start.5 = (f32[2,48,128]{2,1,0:T(8,128)S(1)}, f32[2,48,128]{2,1,0:T(8,128)S(1)}, u32[]{:S(2)}, u32[]{:S(2)}) collective-permute-start(f32[2,48,128]{2,1,0:T(8,128)S(1)} %pad_maximum_fusion.1), channel_id=1, source_target_pairs={{0,5},{1,4},{2,7},{3,6},{4,1},{5,0},{6,3},{7,2},{8,13},{9,12},{10,... | collective-permute-start | bytes 147464 | tf_op jit(solution)/shard_map/ppermute | solution.py:213
  8.6 3.5 %collective-permute-start.2 = (f32[2,48,128]{2,1,0:T(8,128)S(1)}, f32[2,48,128]{2,1,0:T(8,128)S(1)}, u32[]{:S(2)}, u32[]{:S(2)}) collective-permute-start(f32[2,48,128]{2,1,0:T(8,128)S(1)} %pad_maximum_fusion), channel_id=1, source_target_pairs={{0,3},{1,2},{2,1},{3,0},{4,7},{5,6},{6,5},{7,4},{8,11},{9,10},{10,... | collective-permute-start | bytes 147464 | tf_op jit(solution)/shard_map/ppermute | solution.py:213
  12.6 3.2 %collective-permute-start.7 = (f32[2,15,128]{2,1,0:T(8,128)S(1)}, f32[2,15,128]{2,1,0:T(8,128)S(1)}, u32[]{:S(2)}, u32[]{:S(2)}) collective-permute-start(f32[2,15,128]{2,1,0:T(8,128)S(1)} %get-tuple-element.24), channel_id=1, source_target_pairs={{0,9},{1,8},{2,11},{3,10},{4,13},{5,12},{6,15},{7,14},{8,1},{9,0},... | collective-permute-start | bytes 46088 | tf_op jit(solution)/shard_map/ppermute | solution.py:225
  15.8 4.1 %collective-permute-start.8 = (f32[2,15,128]{2,1,0:T(8,128)S(1)}, f32[2,15,128]{2,1,0:T(8,128)S(1)}, u32[]{:S(2)}, u32[]{:S(2)}) collective-permute-start(f32[2,15,128]{2,1,0:T(8,128)S(1)} %pad_maximum_fusion.2), channel_id=1, source_target_pairs={{0,17},{1,16},{2,19},{3,18},{4,21},{5,20},{6,23},{7,22},{8,25},{9,... | collective-permute-start | bytes 46088 | tf_op jit(solution)/shard_map/ppermute | solution.py:225
  15.9 5.3 %collective-permute-start.6 = (f32[180,128]{1,0:T(8,128)S(1)}, f32[180,128]{1,0:T(8,128)S(1)}, u32[]{:S(2)}, u32[]{:S(2)}) collective-permute-start(f32[180,128]{1,0:T(8,128)S(1)} %get-tuple-element.23.own_ref), channel_id=1, source_target_pairs={{0,1},{1,0},{2,3},{3,2},{4,5},{5,4},{6,7},{7,6},{8,9},{9,8},{10,11... | collective-permute-start | bytes 276488 | tf_op jit(solution)/shard_map/ppermute | solution.py:221
  20.0 1.2 %collective-permute-start = (f32[2,15,128]{2,1,0:T(8,128)S(1)}, f32[2,15,128]{2,1,0:T(8,128)S(1)}, u32[]{:S(2)}, u32[]{:S(2)}) collective-permute-start(f32[2,15,128]{2,1,0:T(8,128)S(1)} %param.1), channel_id=1, source_target_pairs={{0,1},{1,0},{2,3},{3,2},{4,5},{5,4},{6,7},{7,6},{8,9},{9,8},{10,11... | collective-permute-start | bytes 46088 | tf_op jit(solution)/shard_map/cond/branch_1_fun/ppermute | solution.py:228

commit v6 on v5

--- a/solution.py
+++ b/solution.py
@@ -214,9 +214,9 @@
     landed = arrivals[0][0]
     forwarded = (lax.ppermute(landed, "reg", swap), (1,))
     sums = bin_some(members, chunks, [(same, (0,)), (partner, (0,))])
-    for n, arrival in enumerate(arrivals):
-        taken = [(landed, (0,))] if n == 0 else [arrival, forwarded] if n == 2 else [arrival]
-        sums = bin_some(members, chunks, taken, sums, n == chips - 2)
+    sums = bin_some(members, chunks, [(landed, (0,))], sums)
+    sums = bin_some(members, chunks, [forwarded], sums)
+    sums = bin_some(members, chunks, arrivals[1:], sums, True)
     moments, own = sums
     passed = lax.ppermute(own, "reg", swap)
     each, reach = members, 1

time: 22.1 us -> 22.2 us (level)
  the two profiles are of different devices: /device:TPU:17 before, /device:TPU:9 now
where the time goes in v6:
time: 22.2 us; the launch traced here: 22 us
  waiting for transfers between devices  9.2 us (41%)
  starting transfers between devices  8.85 us (40%)
  Pallas kernels  3.19 us (14%)
  between operations  0.69 us (3%)
    ppermute x3, starting transfers between devices, step(): arrivals.append((lax.ppermute(sent, 'reg', pairs), (0, 1)))  4.93 us
    ppermute x2, waiting for transfers between devices, step(): theirs = lax.ppermute(moments, ('mem', 'reg'), pairs)  4.39 us
    ppermute x3, waiting for transfers between devices, step(): arrivals.append((lax.ppermute(sent, 'reg', pairs), (0, 1)))  3.7 us
    ppermute x2, starting transfers between devices, step(): theirs = lax.ppermute(moments, ('mem', 'reg'), pairs)  2.53 us
    pallas_call x4, Pallas kernels, bin_some(): pl.pallas_call(body, out_shape=[pltpu.VMEM((2, LINES, LANES), jnp.float32...  1.45 us
    ppermute x1, waiting for transfers between devices, step(): lax.ppermute(m, 'reg', swap)  1.1 us
    pallas_call x1, Pallas kernels, step(): pl.pallas_call(functools.partial(pack_kernel, members, regions, chunks),...  1.05 us
    ppermute x1, starting transfers between devices, step(): partner = lax.ppermute(other, 'reg', swap)  0.74 us
  transfers between devices with their start and end apart: 9, of which 6 were waited for; matrix products, arithmetic and copies ran while one was open for 0% of the time, Pallas kernels for 4%

profile of v6, /device:TPU:9, one launch (start us, length us, event | category | flops | bytes accessed | tf_op | source)
XLA Modules:
  0.0 22.0 jit_solution(5688548040578279464)
XLA Ops:
  0.6 1.1 %shard_map.83 = (f32[3,48,128]{2,1,0:T(8,128)S(1)}, f32[3,48,128]{2,1,0:T(8,128)S(1)}, f32[2,48,128]{2,1,0:T(8,128)S(1)}) custom-call(f32[10,4096]{1,0:T(8,128)} %value_ref.1, f32[32,128]{1,0:T(8,128)} %bitcast.7, f32[32,128]{1,0:T(8,128)} %bitcast.8, s32[32,128]{1,0:T(8,128)} %bitcast.9), custom_call_target="tpu_custom_call" | custom-call | tf_op jit(solution)/shard_map/pallas_call | solution.py:204
  1.7 0.7 %collective-permute-start.1 = (f32[3,48,128]{2,1,0:T(8,128)S(1)}, f32[3,48,128]{2,1,0:T(8,128)S(1)}, u32[]{:S(2)}, u32[]{:S(2)}) collective-permute-start(f32[3,48,128]{2,1,0:T(8,128)S(1)} %get-tuple-element.21), channel_id=1, source_target_pairs={{0,1},{1,0},{2,3},{3,2},{4,5},{5,4},{6,7},{7,6},{8,9},{9,8},{10,11... | collective-permute-start | bytes 221192 | tf_op jit(solution)/shard_map/ppermute | solution.py:208
  2.4 2.1 %collective-permute-start.4 = (f32[2,48,128]{2,1,0:T(8,128)S(1)}, f32[2,48,128]{2,1,0:T(8,128)S(1)}, u32[]{:S(2)}, u32[]{:S(2)}) collective-permute-start(f32[2,48,128]{2,1,0:T(8,128)S(1)} %get-tuple-element.22), channel_id=1, source_target_pairs={{0,7},{1,6},{2,5},{3,4},{4,3},{5,2},{6,1},{7,0},{8,15},{9,14},{10,... | collective-permute-start | bytes 147464 | tf_op jit(solution)/shard_map/ppermute | solution.py:213
  4.6 2.3 %collective-permute-done.4.refs_0_ = f32[2,48,128]{2,1,0:T(8,128)S(1)} collective-permute-done((f32[2,48,128]{2,1,0:T(8,128)S(1)}, f32[2,48,128]{2,1,0:T(8,128)S(1)}, u32[]{:S(2)}, u32[]{:S(2)}) %collective-permute-start.4) | collective-permute-done | bytes 49184 | tf_op jit(solution)/shard_map/ppermute | solution.py:213
  6.8 0.1 collective-permute-start.5
  6.9 0.0 collective-permute-done.1.refs_1_
  6.9 1.6 %collective-permute-start.3 = (f32[2,48,128]{2,1,0:T(8,128)S(1)}, f32[2,48,128]{2,1,0:T(8,128)S(1)}, u32[]{:S(2)}, u32[]{:S(2)}) collective-permute-start(f32[2,48,128]{2,1,0:T(8,128)S(1)} %pad_maximum_fusion.1), channel_id=1, source_target_pairs={{0,3},{1,2},{2,1},{3,0},{4,7},{5,6},{6,5},{7,4},{8,11},{9,10},{10,... | collective-permute-start | bytes 147464 | tf_op jit(solution)/shard_map/ppermute | solution.py:213
  8.5 1.2 %collective-permute-start.2 = (f32[2,48,128]{2,1,0:T(8,128)S(1)}, f32[2,48,128]{2,1,0:T(8,128)S(1)}, u32[]{:S(2)}, u32[]{:S(2)}) collective-permute-start(f32[2,48,128]{2,1,0:T(8,128)S(1)} %pad_maximum_fusion), channel_id=1, source_target_pairs={{0,5},{1,4},{2,7},{3,6},{4,1},{5,0},{6,3},{7,2},{8,13},{9,12},{10,... | collective-permute-start | bytes 147464 | tf_op jit(solution)/shard_map/ppermute | solution.py:213
  9.7 0.3 %shard_map.84.refs_1_ = f32[192,256]{1,0:T(8,128)S(1)} custom-call(f32[3,48,128]{2,1,0:T(8,128)S(1)} %get-tuple-element.20.refs_0_, f32[3,48,128]{2,1,0:T(8,128)S(1)} %collective-permute-done.1.refs_1_), custom_call_target="tpu_custom_call" | custom-call | tf_op jit(solution)/shard_map/pallas_call | solution.py:149
  10.1 0.3 %shard_map.85.refs_1_ = f32[192,256]{1,0:T(8,128)S(1)} custom-call(f32[2,48,128]{2,1,0:T(8,128)S(1)} %collective-permute-done.4.refs_0_, f32[192,256]{1,0:T(8,128)S(1)} %shard_map.84.refs_1_), custom_call_target="tpu_custom_call" | custom-call | tf_op jit(solution)/shard_map/pallas_call | solution.py:149
  10.4 0.0 collective-permute-done.5.refs_0_
  10.4 0.3 %shard_map.86.refs_2_ = f32[192,256]{1,0:T(8,128)S(1)} custom-call(f32[2,48,128]{2,1,0:T(8,128)S(1)} %collective-permute-done.5.refs_0_, f32[192,256]{1,0:T(8,128)S(1)} %shard_map.85.refs_1_), custom_call_target="tpu_custom_call" | custom-call | tf_op jit(solution)/shard_map/pallas_call | solution.py:149
  10.6 0.2 collective-permute-done.3.refs_1_
  10.8 1.2 %collective-permute-done.2.refs_0_ = f32[2,48,128]{2,1,0:T(8,128)S(1)} collective-permute-done((f32[2,48,128]{2,1,0:T(8,128)S(1)}, f32[2,48,128]{2,1,0:T(8,128)S(1)}, u32[]{:S(2)}, u32[]{:S(2)}) %collective-permute-start.2) | collective-permute-done | bytes 49184 | tf_op jit(solution)/shard_map/ppermute | solution.py:213
  12.1 0.6 %shard_map.87 = (f32[2,15,128]{2,1,0:T(8,128)S(1)}, f32[180,128]{1,0:T(8,128)S(1)}) custom-call(f32[2,48,128]{2,1,0:T(8,128)S(1)} %collective-permute-done.2.refs_0_, f32[2,48,128]{2,1,0:T(8,128)S(1)} %collective-permute-done.3.refs_1_, f32[192,256]{1,0:T(8,128)S(1)} %shard_map.86.refs_2_), custom_call_target="tpu_custom_call" | custom-call | tf_op jit(solution)/shard_map/pallas_call | solution.py:149
  12.6 0.2 collective-permute-start.7
  12.8 3.0 %collective-permute-done.7 = f32[2,15,128]{2,1,0:T(8,128)S(1)} collective-permute-done((f32[2,15,128]{2,1,0:T(8,128)S(1)}, f32[2,15,128]{2,1,0:T(8,128)S(1)}, u32[]{:S(2)}, u32[]{:S(2)}) %collective-permute-start.7) | collective-permute-done | bytes 15392 | tf_op jit(solution)/shard_map/ppermute | solution.py:225
  15.9 2.3 %collective-permute-start.8 = (f32[2,15,128]{2,1,0:T(8,128)S(1)}, f32[2,15,128]{2,1,0:T(8,128)S(1)}, u32[]{:S(2)}, u32[]{:S(2)}) collective-permute-start(f32[2,15,128]{2,1,0:T(8,128)S(1)} %pad_maximum_fusion.2), channel_id=1, source_target_pairs={{0,17},{1,16},{2,19},{3,18},{4,21},{5,20},{6,23},{7,22},{8,25},{9,... | collective-permute-start | bytes 46088 | tf_op jit(solution)/shard_map/ppermute | solution.py:225
  18.2 0.4 %collective-permute-start.6 = (f32[180,128]{1,0:T(8,128)S(1)}, f32[180,128]{1,0:T(8,128)S(1)}, u32[]{:S(2)}, u32[]{:S(2)}) collective-permute-start(f32[180,128]{1,0:T(8,128)S(1)} %get-tuple-element.23.own_ref), channel_id=1, source_target_pairs={{0,1},{1,0},{2,3},{3,2},{4,5},{5,4},{6,7},{7,6},{8,9},{9,8},{10,11... | collective-permute-start | bytes 276488 | tf_op jit(solution)/shard_map/ppermute | solution.py:221
  18.7 1.4 %collective-permute-done.8 = f32[2,15,128]{2,1,0:T(8,128)S(1)} collective-permute-done((f32[2,15,128]{2,1,0:T(8,128)S(1)}, f32[2,15,128]{2,1,0:T(8,128)S(1)}, u32[]{:S(2)}, u32[]{:S(2)}) %collective-permute-start.8) | collective-permute-done | bytes 15392 | tf_op jit(solution)/shard_map/ppermute | solution.py:225
  20.0 1.3 %conditional.1 = (f32[2,15,128]{2,1,0:T(8,128)S(1)}) conditional(s32[]{:T(128)} %convert_element_type.3, f32[2,15,128]{2,1,0:T(8,128)S(1)} %pad_maximum_fusion.3, f32[2,15,128]{2,1,0:T(8,128)S(1)} %pad_maximum_fusion.3), branch_computations={%region_0.0_spmd, %region_1.0_spmd} | conditional | bytes 92208 | solution.py:228
  20.1 0.1 collective-permute-start
  20.2 1.1 %collective-permute-done = f32[2,15,128]{2,1,0:T(8,128)S(1)} collective-permute-done((f32[2,15,128]{2,1,0:T(8,128)S(1)}, f32[2,15,128]{2,1,0:T(8,128)S(1)}, u32[]{:S(2)}, u32[]{:S(2)}) %collective-permute-start) | collective-permute-done | bytes 15392 | tf_op jit(solution)/shard_map/cond/branch_1_fun/ppermute | solution.py:228
  21.3 0.0 collective-permute-done.6.passed_ref
  21.3 0.7 %shard_map.88 = (f32[10,1920]{1,0:T(8,128)}, f32[15,128]{1,0:T(8,128)}, f32[15,128]{1,0:T(8,128)}, f32[15,128]{1,0:T(8,128)}, s32[15,128]{1,0:T(8,128)}) custom-call(f32[180,128]{1,0:T(8,128)S(1)} %get-tuple-element.23.own_ref, f32[180,128]{1,0:T(8,128)S(1)} %collective-permute-done.6.passed_ref, f32[2,15,128]{2,1,0:T(8,128)S(1)} %get-tuple-element.38.moment_ref), custom_call_target="tpu_custom_call" | custom-call | tf_op jit(solution)/shard_map/pallas_call | solution.py:230
  (9 shorter events, 0.0 us)
Async XLA Ops:
  1.7 5.2 %collective-permute-start.1 = (f32[3,48,128]{2,1,0:T(8,128)S(1)}, f32[3,48,128]{2,1,0:T(8,128)S(1)}, u32[]{:S(2)}, u32[]{:S(2)}) collective-permute-start(f32[3,48,128]{2,1,0:T(8,128)S(1)} %get-tuple-element.21), channel_id=1, source_target_pairs={{0,1},{1,0},{2,3},{3,2},{4,5},{5,4},{6,7},{7,6},{8,9},{9,8},{10,11... | collective-permute-start | bytes 221192 | tf_op jit(solution)/shard_map/ppermute | solution.py:208
  2.4 4.4 %collective-permute-start.4 = (f32[2,48,128]{2,1,0:T(8,128)S(1)}, f32[2,48,128]{2,1,0:T(8,128)S(1)}, u32[]{:S(2)}, u32[]{:S(2)}) collective-permute-start(f32[2,48,128]{2,1,0:T(8,128)S(1)} %get-tuple-element.22), channel_id=1, source_target_pairs={{0,7},{1,6},{2,5},{3,4},{4,3},{5,2},{6,1},{7,0},{8,15},{9,14},{10,... | collective-permute-start | bytes 147464 | tf_op jit(solution)/shard_map/ppermute | solution.py:213
  6.8 3.5 %collective-permute-start.5 = (f32[2,48,128]{2,1,0:T(8,128)S(1)}, f32[2,48,128]{2,1,0:T(8,128)S(1)}, u32[]{:S(2)}, u32[]{:S(2)}) collective-permute-start(f32[2,48,128]{2,1,0:T(8,128)S(1)} %collective-permute-done.4.refs_0_), channel_id=1, source_target_pairs={{0,1},{1,0},{2,3},{3,2},{4,5},{5,4},{6,7},{7,6},{8,9},{9,8},{10,11... | collective-permute-start | bytes 147464 | tf_op jit(solution)/shard_map/ppermute | solution.py:215
  6.9 3.9 %collective-permute-start.3 = (f32[2,48,128]{2,1,0:T(8,128)S(1)}, f32[2,48,128]{2,1,0:T(8,128)S(1)}, u32[]{:S(2)}, u32[]{:S(2)}) collective-permute-start(f32[2,48,128]{2,1,0:T(8,128)S(1)} %pad_maximum_fusion.1), channel_id=1, source_target_pairs={{0,3},{1,2},{2,1},{3,0},{4,7},{5,6},{6,5},{7,4},{8,11},{9,10},{10,... | collective-permute-start | bytes 147464 | tf_op jit(solution)/shard_map/ppermute | solution.py:213
  8.5 3.5 %collective-permute-start.2 = (f32[2,48,128]{2,1,0:T(8,128)S(1)}, f32[2,48,128]{2,1,0:T(8,128)S(1)}, u32[]{:S(2)}, u32[]{:S(2)}) collective-permute-start(f32[2,48,128]{2,1,0:T(8,128)S(1)} %pad_maximum_fusion), channel_id=1, source_target_pairs={{0,5},{1,4},{2,7},{3,6},{4,1},{5,0},{6,3},{7,2},{8,13},{9,12},{10,... | collective-permute-start | bytes 147464 | tf_op jit(solution)/shard_map/ppermute | solution.py:213
  12.6 3.2 %collective-permute-start.7 = (f32[2,15,128]{2,1,0:T(8,128)S(1)}, f32[2,15,128]{2,1,0:T(8,128)S(1)}, u32[]{:S(2)}, u32[]{:S(2)}) collective-permute-start(f32[2,15,128]{2,1,0:T(8,128)S(1)} %get-tuple-element.24), channel_id=1, source_target_pairs={{0,9},{1,8},{2,11},{3,10},{4,13},{5,12},{6,15},{7,14},{8,1},{9,0},... | collective-permute-start | bytes 46088 | tf_op jit(solution)/shard_map/ppermute | solution.py:225
  15.9 4.1 %collective-permute-start.8 = (f32[2,15,128]{2,1,0:T(8,128)S(1)}, f32[2,15,128]{2,1,0:T(8,128)S(1)}, u32[]{:S(2)}, u32[]{:S(2)}) collective-permute-start(f32[2,15,128]{2,1,0:T(8,128)S(1)} %pad_maximum_fusion.2), channel_id=1, source_target_pairs={{0,17},{1,16},{2,19},{3,18},{4,21},{5,20},{6,23},{7,22},{8,25},{9,... | collective-permute-start | bytes 46088 | tf_op jit(solution)/shard_map/ppermute | solution.py:225
  18.2 3.1 %collective-permute-start.6 = (f32[180,128]{1,0:T(8,128)S(1)}, f32[180,128]{1,0:T(8,128)S(1)}, u32[]{:S(2)}, u32[]{:S(2)}) collective-permute-start(f32[180,128]{1,0:T(8,128)S(1)} %get-tuple-element.23.own_ref), channel_id=1, source_target_pairs={{0,1},{1,0},{2,3},{3,2},{4,5},{5,4},{6,7},{7,6},{8,9},{9,8},{10,11... | collective-permute-start | bytes 276488 | tf_op jit(solution)/shard_map/ppermute | solution.py:221
  20.1 1.2 %collective-permute-start = (f32[2,15,128]{2,1,0:T(8,128)S(1)}, f32[2,15,128]{2,1,0:T(8,128)S(1)}, u32[]{:S(2)}, u32[]{:S(2)}) collective-permute-start(f32[2,15,128]{2,1,0:T(8,128)S(1)} %param.1), channel_id=1, source_target_pairs={{0,1},{1,0},{2,3},{3,2},{4,5},{5,4},{6,7},{7,6},{8,9},{9,8},{10,11... | collective-permute-start | bytes 46088 | tf_op jit(solution)/shard_map/cond/branch_1_fun/ppermute | solution.py:228

commit v7 on v6

--- a/solution.py
+++ b/solution.py
@@ -159,7 +159,7 @@
 
 
 def final_kernel(
-    members, total, own_ref, passed_ref, moment_ref, out_ref, departure_ref, variance_ref, error_ref, count_ref
+    members, total, own_ref, passed_ref, moment_ref, own_count_ref, out_ref, departure_ref, variance_ref, error_ref, count_ref
 ):
     mean = moment_ref[0] * (1.0 / total)
     departure_ref[...] = -mean
@@ -168,7 +168,9 @@
     rows, whole = block_rows(members)
     rest, extra = rows - whole, members - whole
 
-    def write(result_ref):
+    def write(result_ref, own_counts=None):
+        if own_counts is not None:
+            count_ref[...] = own_counts[...]
         for j in range(LINES):
             cut = slice(j * LANES, (j + 1) * LANES)
             tail = LINES * whole + j * rest
@@ -176,11 +178,19 @@
             out_ref[:whole, cut] = result_ref[j * whole : (j + 1) * whole, :] - line
             out_ref[whole:, cut] = result_ref[tail : tail + extra, :] - line
             error_ref[j : j + 1, :] = result_ref[below, :]
-            count_ref[j : j + 1, :] = result_ref[tail + extra + 1 : tail + extra + 2, :].astype(jnp.int32)
+            if own_counts is None:
+                count_ref[j : j + 1, :] = result_ref[tail + extra + 1 : tail + extra + 2, :].astype(jnp.int32)
 
     odd = odd_plane()
-    pl.when(odd == 0)(lambda: write(own_ref))
+    pl.when(odd == 0)(lambda: write(own_ref, own_count_ref))
     pl.when(odd == 1)(lambda: write(passed_ref))
+
+
+def count_kernel(members, result_ref, out_ref):
+    rows, whole = block_rows(members)
+    for j in range(LINES):
+        spot = LINES * whole + (j + 1) * (rows - whole) - 1
+        out_ref[j : j + 1, :] = result_ref[spot : spot + 1, :].astype(jnp.int32)
 
 
 def merge(mine, theirs, each):
@@ -219,6 +229,9 @@
     sums = bin_some(members, chunks, arrivals[1:], sums, True)
     moments, own = sums
     passed = lax.ppermute(own, "reg", swap)
+    counts = pl.pallas_call(
+        functools.partial(count_kernel, members), out_shape=pltpu.VMEM((LINES, LANES), jnp.int32)
+    )(near(own))
     each, reach = members, 1
     while reach < groups:
         pairs = [(z * regions + i, (z ^ reach) * regions + (i ^ 1)) for z in range(groups) for i in range(regions)]
@@ -236,7 +249,7 @@
             cells,
             jax.ShapeDtypeStruct((LINES, LANES), jnp.int32),
         ],
-    )(*[near(a) for a in (own, passed, moments)])
+    )(*[near(a) for a in (own, passed, moments, counts)])
     return (outs[0], *[out.reshape(-1) for out in outs[1:]])
 
 

time: 22.2 us -> 22.2 us (level)
  no operation moved by 1% of the time
where the time goes in v7:
time: 22.2 us; the launch traced here: 22 us
  waiting for transfers between devices  9.19 us (41%)
  starting transfers between devices  8.85 us (40%)
  Pallas kernels  3.2 us (14%)
  between operations  0.69 us (3%)
    ppermute x3, starting transfers between devices, step(): arrivals.append((lax.ppermute(sent, 'reg', pairs), (0, 1)))  4.93 us
    ppermute x2, waiting for transfers between devices, step(): theirs = lax.ppermute(moments, ('mem', 'reg'), pairs)  4.39 us
    ppermute x3, waiting for transfers between devices, step(): arrivals.append((lax.ppermute(sent, 'reg', pairs), (0, 1)))  3.7 us
    ppermute x2, starting transfers between devices, step(): theirs = lax.ppermute(moments, ('mem', 'reg'), pairs)  2.53 us
    pallas_call x4, Pallas kernels, bin_some(): pl.pallas_call(body, out_shape=[pltpu.VMEM((2, LINES, LANES), jnp.float32...  1.45 us
    ppermute x1, waiting for transfers between devices, step(): lax.ppermute(m, 'reg', swap)  1.1 us
    pallas_call x1, Pallas kernels, step(): pl.pallas_call(functools.partial(pack_kernel, members, regions, chunks),...  1.05 us
    ppermute x1, starting transfers between devices, step(): partner = lax.ppermute(other, 'reg', swap)  0.74 us
  transfers between devices with their start and end apart: 9, of which 6 were waited for; matrix products, arithmetic and copies ran while one was open for 0% of the time, Pallas kernels for 4%

profile of v7, /device:TPU:9, one launch (start us, length us, event | category | flops | bytes accessed | tf_op | source)
XLA Modules:
  0.0 22.0 jit_solution(3315368506196651314)
XLA Ops:
  0.6 1.1 %shard_map.83 = (f32[3,48,128]{2,1,0:T(8,128)S(1)}, f32[3,48,128]{2,1,0:T(8,128)S(1)}, f32[2,48,128]{2,1,0:T(8,128)S(1)}) custom-call(f32[10,4096]{1,0:T(8,128)} %value_ref.1, f32[32,128]{1,0:T(8,128)} %bitcast.7, f32[32,128]{1,0:T(8,128)} %bitcast.8, s32[32,128]{1,0:T(8,128)} %bitcast.9), custom_call_target="tpu_custom_call" | custom-call | tf_op jit(solution)/shard_map/pallas_call | solution.py:214
  1.7 0.7 %collective-permute-start.1 = (f32[3,48,128]{2,1,0:T(8,128)S(1)}, f32[3,48,128]{2,1,0:T(8,128)S(1)}, u32[]{:S(2)}, u32[]{:S(2)}) collective-permute-start(f32[3,48,128]{2,1,0:T(8,128)S(1)} %get-tuple-element.21), channel_id=1, source_target_pairs={{0,1},{1,0},{2,3},{3,2},{4,5},{5,4},{6,7},{7,6},{8,9},{9,8},{10,11... | collective-permute-start | bytes 221192 | tf_op jit(solution)/shard_map/ppermute | solution.py:218
  2.4 2.1 %collective-permute-start.4 = (f32[2,48,128]{2,1,0:T(8,128)S(1)}, f32[2,48,128]{2,1,0:T(8,128)S(1)}, u32[]{:S(2)}, u32[]{:S(2)}) collective-permute-start(f32[2,48,128]{2,1,0:T(8,128)S(1)} %get-tuple-element.22), channel_id=1, source_target_pairs={{0,7},{1,6},{2,5},{3,4},{4,3},{5,2},{6,1},{7,0},{8,15},{9,14},{10,... | collective-permute-start | bytes 147464 | tf_op jit(solution)/shard_map/ppermute | solution.py:223
  4.6 2.3 %collective-permute-done.4.refs_0_ = f32[2,48,128]{2,1,0:T(8,128)S(1)} collective-permute-done((f32[2,48,128]{2,1,0:T(8,128)S(1)}, f32[2,48,128]{2,1,0:T(8,128)S(1)}, u32[]{:S(2)}, u32[]{:S(2)}) %collective-permute-start.4) | collective-permute-done | bytes 49184 | tf_op jit(solution)/shard_map/ppermute | solution.py:223
  6.8 0.1 collective-permute-start.5
  6.9 0.0 collective-permute-done.1.refs_1_
  6.9 1.6 %collective-permute-start.3 = (f32[2,48,128]{2,1,0:T(8,128)S(1)}, f32[2,48,128]{2,1,0:T(8,128)S(1)}, u32[]{:S(2)}, u32[]{:S(2)}) collective-permute-start(f32[2,48,128]{2,1,0:T(8,128)S(1)} %pad_maximum_fusion.1), channel_id=1, source_target_pairs={{0,3},{1,2},{2,1},{3,0},{4,7},{5,6},{6,5},{7,4},{8,11},{9,10},{10,... | collective-permute-start | bytes 147464 | tf_op jit(solution)/shard_map/ppermute | solution.py:223
  8.5 1.2 %collective-permute-start.2 = (f32[2,48,128]{2,1,0:T(8,128)S(1)}, f32[2,48,128]{2,1,0:T(8,128)S(1)}, u32[]{:S(2)}, u32[]{:S(2)}) collective-permute-start(f32[2,48,128]{2,1,0:T(8,128)S(1)} %pad_maximum_fusion), channel_id=1, source_target_pairs={{0,5},{1,4},{2,7},{3,6},{4,1},{5,0},{6,3},{7,2},{8,13},{9,12},{10,... | collective-permute-start | bytes 147464 | tf_op jit(solution)/shard_map/ppermute | solution.py:223
  9.7 0.3 %shard_map.84.refs_1_ = f32[192,256]{1,0:T(8,128)S(1)} custom-call(f32[3,48,128]{2,1,0:T(8,128)S(1)} %get-tuple-element.20.refs_0_, f32[3,48,128]{2,1,0:T(8,128)S(1)} %collective-permute-done.1.refs_1_), custom_call_target="tpu_custom_call" | custom-call | tf_op jit(solution)/shard_map/pallas_call | solution.py:149
  10.1 0.3 %shard_map.85.refs_1_ = f32[192,256]{1,0:T(8,128)S(1)} custom-call(f32[2,48,128]{2,1,0:T(8,128)S(1)} %collective-permute-done.4.refs_0_, f32[192,256]{1,0:T(8,128)S(1)} %shard_map.84.refs_1_), custom_call_target="tpu_custom_call" | custom-call | tf_op jit(solution)/shard_map/pallas_call | solution.py:149
  10.4 0.0 collective-permute-done.5.refs_0_
  10.4 0.3 %shard_map.86.refs_2_ = f32[192,256]{1,0:T(8,128)S(1)} custom-call(f32[2,48,128]{2,1,0:T(8,128)S(1)} %collective-permute-done.5.refs_0_, f32[192,256]{1,0:T(8,128)S(1)} %shard_map.85.refs_1_), custom_call_target="tpu_custom_call" | custom-call | tf_op jit(solution)/shard_map/pallas_call | solution.py:149
  10.6 0.2 collective-permute-done.3.refs_1_
  10.8 1.2 %collective-permute-done.2.refs_0_ = f32[2,48,128]{2,1,0:T(8,128)S(1)} collective-permute-done((f32[2,48,128]{2,1,0:T(8,128)S(1)}, f32[2,48,128]{2,1,0:T(8,128)S(1)}, u32[]{:S(2)}, u32[]{:S(2)}) %collective-permute-start.2) | collective-permute-done | bytes 49184 | tf_op jit(solution)/shard_map/ppermute | solution.py:223
  12.1 0.6 %shard_map.87 = (f32[2,15,128]{2,1,0:T(8,128)S(1)}, f32[180,128]{1,0:T(8,128)S(1)}) custom-call(f32[2,48,128]{2,1,0:T(8,128)S(1)} %collective-permute-done.2.refs_0_, f32[2,48,128]{2,1,0:T(8,128)S(1)} %collective-permute-done.3.refs_1_, f32[192,256]{1,0:T(8,128)S(1)} %shard_map.86.refs_2_), custom_call_target="tpu_custom_call" | custom-call | tf_op jit(solution)/shard_map/pallas_call | solution.py:149
  12.6 0.2 collective-permute-start.7
  12.8 3.0 %collective-permute-done.7 = f32[2,15,128]{2,1,0:T(8,128)S(1)} collective-permute-done((f32[2,15,128]{2,1,0:T(8,128)S(1)}, f32[2,15,128]{2,1,0:T(8,128)S(1)}, u32[]{:S(2)}, u32[]{:S(2)}) %collective-permute-start.7) | collective-permute-done | bytes 15392 | tf_op jit(solution)/shard_map/ppermute | solution.py:238
  15.9 2.3 %collective-permute-start.8 = (f32[2,15,128]{2,1,0:T(8,128)S(1)}, f32[2,15,128]{2,1,0:T(8,128)S(1)}, u32[]{:S(2)}, u32[]{:S(2)}) collective-permute-start(f32[2,15,128]{2,1,0:T(8,128)S(1)} %pad_maximum_fusion.2), channel_id=1, source_target_pairs={{0,17},{1,16},{2,19},{3,18},{4,21},{5,20},{6,23},{7,22},{8,25},{9,... | collective-permute-start | bytes 46088 | tf_op jit(solution)/shard_map/ppermute | solution.py:238
  18.2 0.4 %collective-permute-start.6 = (f32[180,128]{1,0:T(8,128)S(1)}, f32[180,128]{1,0:T(8,128)S(1)}, u32[]{:S(2)}, u32[]{:S(2)}) collective-permute-start(f32[180,128]{1,0:T(8,128)S(1)} %get-tuple-element.23.result_ref.own_ref), channel_id=1, source_target_pairs={{0,1},{1,0},{2,3},{3,2},{4,5},{5,4},{6,7},{7,6},{8,9},{9,8},{10,11... | collective-permute-start | bytes 276488 | tf_op jit(solution)/shard_map/ppermute | solution.py:231
  18.7 1.4 %collective-permute-done.8 = f32[2,15,128]{2,1,0:T(8,128)S(1)} collective-permute-done((f32[2,15,128]{2,1,0:T(8,128)S(1)}, f32[2,15,128]{2,1,0:T(8,128)S(1)}, u32[]{:S(2)}, u32[]{:S(2)}) %collective-permute-start.8) | collective-permute-done | bytes 15392 | tf_op jit(solution)/shard_map/ppermute | solution.py:238
  20.0 1.3 %conditional.1 = (f32[2,15,128]{2,1,0:T(8,128)S(1)}) conditional(s32[]{:T(128)} %convert_element_type.3, f32[2,15,128]{2,1,0:T(8,128)S(1)} %pad_maximum_fusion.3, f32[2,15,128]{2,1,0:T(8,128)S(1)} %pad_maximum_fusion.3), branch_computations={%region_0.0_spmd, %region_1.0_spmd} | conditional | bytes 92208 | solution.py:241
  20.1 0.1 collective-permute-start
  20.2 1.1 %collective-permute-done = f32[2,15,128]{2,1,0:T(8,128)S(1)} collective-permute-done((f32[2,15,128]{2,1,0:T(8,128)S(1)}, f32[2,15,128]{2,1,0:T(8,128)S(1)}, u32[]{:S(2)}, u32[]{:S(2)}) %collective-permute-start) | collective-permute-done | bytes 15392 | tf_op jit(solution)/shard_map/cond/branch_1_fun/ppermute | solution.py:241
  21.3 0.0 collective-permute-done.6.passed_ref
  21.3 0.7 %shard_map.89 = (f32[10,1920]{1,0:T(8,128)}, f32[15,128]{1,0:T(8,128)}, f32[15,128]{1,0:T(8,128)}, f32[15,128]{1,0:T(8,128)}, s32[15,128]{1,0:T(8,128)}) custom-call(f32[180,128]{1,0:T(8,128)S(1)} %get-tuple-element.23.result_ref.own_ref, f32[180,128]{1,0:T(8,128)S(1)} %collective-permute-done.6.passed_ref, f32[2,15,128]{2,1,0:T(8,128)S(1)} %get-tuple-element.38.moment_ref, ...), custom_call_target="tpu_custom_call" | custom-call | tf_op jit(solution)/shard_map/pallas_call | solution.py:243
  (10 shorter events, 0.1 us)
Async XLA Ops:
  1.7 5.2 %collective-permute-start.1 = (f32[3,48,128]{2,1,0:T(8,128)S(1)}, f32[3,48,128]{2,1,0:T(8,128)S(1)}, u32[]{:S(2)}, u32[]{:S(2)}) collective-permute-start(f32[3,48,128]{2,1,0:T(8,128)S(1)} %get-tuple-element.21), channel_id=1, source_target_pairs={{0,1},{1,0},{2,3},{3,2},{4,5},{5,4},{6,7},{7,6},{8,9},{9,8},{10,11... | collective-permute-start | bytes 221192 | tf_op jit(solution)/shard_map/ppermute | solution.py:218
  2.4 4.4 %collective-permute-start.4 = (f32[2,48,128]{2,1,0:T(8,128)S(1)}, f32[2,48,128]{2,1,0:T(8,128)S(1)}, u32[]{:S(2)}, u32[]{:S(2)}) collective-permute-start(f32[2,48,128]{2,1,0:T(8,128)S(1)} %get-tuple-element.22), channel_id=1, source_target_pairs={{0,7},{1,6},{2,5},{3,4},{4,3},{5,2},{6,1},{7,0},{8,15},{9,14},{10,... | collective-permute-start | bytes 147464 | tf_op jit(solution)/shard_map/ppermute | solution.py:223
  6.8 3.5 %collective-permute-start.5 = (f32[2,48,128]{2,1,0:T(8,128)S(1)}, f32[2,48,128]{2,1,0:T(8,128)S(1)}, u32[]{:S(2)}, u32[]{:S(2)}) collective-permute-start(f32[2,48,128]{2,1,0:T(8,128)S(1)} %collective-permute-done.4.refs_0_), channel_id=1, source_target_pairs={{0,1},{1,0},{2,3},{3,2},{4,5},{5,4},{6,7},{7,6},{8,9},{9,8},{10,11... | collective-permute-start | bytes 147464 | tf_op jit(solution)/shard_map/ppermute | solution.py:225
  6.9 3.9 %collective-permute-start.3 = (f32[2,48,128]{2,1,0:T(8,128)S(1)}, f32[2,48,128]{2,1,0:T(8,128)S(1)}, u32[]{:S(2)}, u32[]{:S(2)}) collective-permute-start(f32[2,48,128]{2,1,0:T(8,128)S(1)} %pad_maximum_fusion.1), channel_id=1, source_target_pairs={{0,3},{1,2},{2,1},{3,0},{4,7},{5,6},{6,5},{7,4},{8,11},{9,10},{10,... | collective-permute-start | bytes 147464 | tf_op jit(solution)/shard_map/ppermute | solution.py:223
  8.5 3.5 %collective-permute-start.2 = (f32[2,48,128]{2,1,0:T(8,128)S(1)}, f32[2,48,128]{2,1,0:T(8,128)S(1)}, u32[]{:S(2)}, u32[]{:S(2)}) collective-permute-start(f32[2,48,128]{2,1,0:T(8,128)S(1)} %pad_maximum_fusion), channel_id=1, source_target_pairs={{0,5},{1,4},{2,7},{3,6},{4,1},{5,0},{6,3},{7,2},{8,13},{9,12},{10,... | collective-permute-start | bytes 147464 | tf_op jit(solution)/shard_map/ppermute | solution.py:223
  12.6 3.2 %collective-permute-start.7 = (f32[2,15,128]{2,1,0:T(8,128)S(1)}, f32[2,15,128]{2,1,0:T(8,128)S(1)}, u32[]{:S(2)}, u32[]{:S(2)}) collective-permute-start(f32[2,15,128]{2,1,0:T(8,128)S(1)} %get-tuple-element.24), channel_id=1, source_target_pairs={{0,9},{1,8},{2,11},{3,10},{4,13},{5,12},{6,15},{7,14},{8,1},{9,0},... | collective-permute-start | bytes 46088 | tf_op jit(solution)/shard_map/ppermute | solution.py:238
  15.9 4.1 %collective-permute-start.8 = (f32[2,15,128]{2,1,0:T(8,128)S(1)}, f32[2,15,128]{2,1,0:T(8,128)S(1)}, u32[]{:S(2)}, u32[]{:S(2)}) collective-permute-start(f32[2,15,128]{2,1,0:T(8,128)S(1)} %pad_maximum_fusion.2), channel_id=1, source_target_pairs={{0,17},{1,16},{2,19},{3,18},{4,21},{5,20},{6,23},{7,22},{8,25},{9,... | collective-permute-start | bytes 46088 | tf_op jit(solution)/shard_map/ppermute | solution.py:238
  18.2 3.1 %collective-permute-start.6 = (f32[180,128]{1,0:T(8,128)S(1)}, f32[180,128]{1,0:T(8,128)S(1)}, u32[]{:S(2)}, u32[]{:S(2)}) collective-permute-start(f32[180,128]{1,0:T(8,128)S(1)} %get-tuple-element.23.result_ref.own_ref), channel_id=1, source_target_pairs={{0,1},{1,0},{2,3},{3,2},{4,5},{5,4},{6,7},{7,6},{8,9},{9,8},{10,11... | collective-permute-start | bytes 276488 | tf_op jit(solution)/shard_map/ppermute | solution.py:231
  20.1 1.2 %collective-permute-start = (f32[2,15,128]{2,1,0:T(8,128)S(1)}, f32[2,15,128]{2,1,0:T(8,128)S(1)}, u32[]{:S(2)}, u32[]{:S(2)}) collective-permute-start(f32[2,15,128]{2,1,0:T(8,128)S(1)} %param.1), channel_id=1, source_target_pairs={{0,1},{1,0},{2,3},{3,2},{4,5},{5,4},{6,7},{7,6},{8,9},{9,8},{10,11... | collective-permute-start | bytes 46088 | tf_op jit(solution)/shard_map/cond/branch_1_fun/ppermute | solution.py:241

commit v8 on v7

--- a/solution.py
+++ b/solution.py
@@ -232,12 +232,12 @@
     counts = pl.pallas_call(
         functools.partial(count_kernel, members), out_shape=pltpu.VMEM((LINES, LANES), jnp.int32)
     )(near(own))
-    each, reach = members, 1
-    while reach < groups:
+    each, reach = members, groups // 2
+    while reach:
         pairs = [(z * regions + i, (z ^ reach) * regions + (i ^ 1)) for z in range(groups) for i in range(regions)]
         theirs = lax.ppermute(moments, ("mem", "reg"), pairs)
         moments = merge(moments, theirs, each)
-        each, reach = 2 * each, 2 * reach
+        each, reach = 2 * each, reach // 2
     moments = lax.cond(odd_plane() == 1, lambda m: lax.ppermute(m, "reg", swap), lambda m: m, moments)
     cells = jax.ShapeDtypeStruct((LINES, LANES), jnp.float32)
     outs = pl.pallas_call(

time: 22.2 us -> 22.2 us (level)
  no operation moved by 1% of the time
where the time goes in v8:
time: 22.2 us; the launch traced here: 22 us
  waiting for transfers between devices  9.19 us (41%)
  starting transfers between devices  8.86 us (40%)
  Pallas kernels  3.2 us (14%)
  between operations  0.69 us (3%)
    ppermute x3, starting transfers between devices, step(): arrivals.append((lax.ppermute(sent, 'reg', pairs), (0, 1)))  4.93 us
    ppermute x2, waiting for transfers between devices, step(): theirs = lax.ppermute(moments, ('mem', 'reg'), pairs)  4.38 us
    ppermute x3, waiting for transfers between devices, step(): arrivals.append((lax.ppermute(sent, 'reg', pairs), (0, 1)))  3.7 us
    ppermute x2, starting transfers between devices, step(): theirs = lax.ppermute(moments, ('mem', 'reg'), pairs)  2.54 us
    pallas_call x4, Pallas kernels, bin_some(): pl.pallas_call(body, out_shape=[pltpu.VMEM((2, LINES, LANES), jnp.float32...  1.45 us
    ppermute x1, waiting for transfers between devices, step(): lax.ppermute(m, 'reg', swap)  1.1 us
    pallas_call x1, Pallas kernels, step(): pl.pallas_call(functools.partial(pack_kernel, members, regions, chunks),...  1.05 us
    ppermute x1, starting transfers between devices, step(): partner = lax.ppermute(other, 'reg', swap)  0.74 us
  transfers between devices with their start and end apart: 9, of which 6 were waited for; matrix products, arithmetic and copies ran while one was open for 0% of the time, Pallas kernels for 4%

profile of v8, /device:TPU:9, one launch (start us, length us, event | category | flops | bytes accessed | tf_op | source)
XLA Modules:
  0.0 22.0 jit_solution(10452128338815919908)
XLA Ops:
  0.6 1.1 %shard_map.83 = (f32[3,48,128]{2,1,0:T(8,128)S(1)}, f32[3,48,128]{2,1,0:T(8,128)S(1)}, f32[2,48,128]{2,1,0:T(8,128)S(1)}) custom-call(f32[10,4096]{1,0:T(8,128)} %value_ref.1, f32[32,128]{1,0:T(8,128)} %bitcast.7, f32[32,128]{1,0:T(8,128)} %bitcast.8, s32[32,128]{1,0:T(8,128)} %bitcast.9), custom_call_target="tpu_custom_call" | custom-call | tf_op jit(solution)/shard_map/pallas_call | solution.py:214
  1.7 0.7 %collective-permute-start.1 = (f32[3,48,128]{2,1,0:T(8,128)S(1)}, f32[3,48,128]{2,1,0:T(8,128)S(1)}, u32[]{:S(2)}, u32[]{:S(2)}) collective-permute-start(f32[3,48,128]{2,1,0:T(8,128)S(1)} %get-tuple-element.21), channel_id=1, source_target_pairs={{0,1},{1,0},{2,3},{3,2},{4,5},{5,4},{6,7},{7,6},{8,9},{9,8},{10,11... | collective-permute-start | bytes 221192 | tf_op jit(solution)/shard_map/ppermute | solution.py:218
  2.4 2.1 %collective-permute-start.4 = (f32[2,48,128]{2,1,0:T(8,128)S(1)}, f32[2,48,128]{2,1,0:T(8,128)S(1)}, u32[]{:S(2)}, u32[]{:S(2)}) collective-permute-start(f32[2,48,128]{2,1,0:T(8,128)S(1)} %get-tuple-element.22), channel_id=1, source_target_pairs={{0,7},{1,6},{2,5},{3,4},{4,3},{5,2},{6,1},{7,0},{8,15},{9,14},{10,... | collective-permute-start | bytes 147464 | tf_op jit(solution)/shard_map/ppermute | solution.py:223
  4.6 2.3 %collective-permute-done.4.refs_0_ = f32[2,48,128]{2,1,0:T(8,128)S(1)} collective-permute-done((f32[2,48,128]{2,1,0:T(8,128)S(1)}, f32[2,48,128]{2,1,0:T(8,128)S(1)}, u32[]{:S(2)}, u32[]{:S(2)}) %collective-permute-start.4) | collective-permute-done | bytes 49184 | tf_op jit(solution)/shard_map/ppermute | solution.py:223
  6.8 0.1 collective-permute-start.5
  6.9 0.0 collective-permute-done.1.refs_1_
  6.9 1.6 %collective-permute-start.3 = (f32[2,48,128]{2,1,0:T(8,128)S(1)}, f32[2,48,128]{2,1,0:T(8,128)S(1)}, u32[]{:S(2)}, u32[]{:S(2)}) collective-permute-start(f32[2,48,128]{2,1,0:T(8,128)S(1)} %pad_maximum_fusion.1), channel_id=1, source_target_pairs={{0,3},{1,2},{2,1},{3,0},{4,7},{5,6},{6,5},{7,4},{8,11},{9,10},{10,... | collective-permute-start | bytes 147464 | tf_op jit(solution)/shard_map/ppermute | solution.py:223
  8.5 1.2 %collective-permute-start.2 = (f32[2,48,128]{2,1,0:T(8,128)S(1)}, f32[2,48,128]{2,1,0:T(8,128)S(1)}, u32[]{:S(2)}, u32[]{:S(2)}) collective-permute-start(f32[2,48,128]{2,1,0:T(8,128)S(1)} %pad_maximum_fusion), channel_id=1, source_target_pairs={{0,5},{1,4},{2,7},{3,6},{4,1},{5,0},{6,3},{7,2},{8,13},{9,12},{10,... | collective-permute-start | bytes 147464 | tf_op jit(solution)/shard_map/ppermute | solution.py:223
  9.7 0.3 %shard_map.84.refs_1_ = f32[192,256]{1,0:T(8,128)S(1)} custom-call(f32[3,48,128]{2,1,0:T(8,128)S(1)} %get-tuple-element.20.refs_0_, f32[3,48,128]{2,1,0:T(8,128)S(1)} %collective-permute-done.1.refs_1_), custom_call_target="tpu_custom_call" | custom-call | tf_op jit(solution)/shard_map/pallas_call | solution.py:149
  10.1 0.3 %shard_map.85.refs_1_ = f32[192,256]{1,0:T(8,128)S(1)} custom-call(f32[2,48,128]{2,1,0:T(8,128)S(1)} %collective-permute-done.4.refs_0_, f32[192,256]{1,0:T(8,128)S(1)} %shard_map.84.refs_1_), custom_call_target="tpu_custom_call" | custom-call | tf_op jit(solution)/shard_map/pallas_call | solution.py:149
  10.4 0.0 collective-permute-done.5.refs_0_
  10.4 0.3 %shard_map.86.refs_2_ = f32[192,256]{1,0:T(8,128)S(1)} custom-call(f32[2,48,128]{2,1,0:T(8,128)S(1)} %collective-permute-done.5.refs_0_, f32[192,256]{1,0:T(8,128)S(1)} %shard_map.85.refs_1_), custom_call_target="tpu_custom_call" | custom-call | tf_op jit(solution)/shard_map/pallas_call | solution.py:149
  10.6 0.2 collective-permute-done.3.refs_1_
  10.8 1.2 %collective-permute-done.2.refs_0_ = f32[2,48,128]{2,1,0:T(8,128)S(1)} collective-permute-done((f32[2,48,128]{2,1,0:T(8,128)S(1)}, f32[2,48,128]{2,1,0:T(8,128)S(1)}, u32[]{:S(2)}, u32[]{:S(2)}) %collective-permute-start.2) | collective-permute-done | bytes 49184 | tf_op jit(solution)/shard_map/ppermute | solution.py:223
  12.1 0.6 %shard_map.87 = (f32[2,15,128]{2,1,0:T(8,128)S(1)}, f32[180,128]{1,0:T(8,128)S(1)}) custom-call(f32[2,48,128]{2,1,0:T(8,128)S(1)} %collective-permute-done.2.refs_0_, f32[2,48,128]{2,1,0:T(8,128)S(1)} %collective-permute-done.3.refs_1_, f32[192,256]{1,0:T(8,128)S(1)} %shard_map.86.refs_2_), custom_call_target="tpu_custom_call" | custom-call | tf_op jit(solution)/shard_map/pallas_call | solution.py:149
  12.6 2.3 %collective-permute-start.7 = (f32[2,15,128]{2,1,0:T(8,128)S(1)}, f32[2,15,128]{2,1,0:T(8,128)S(1)}, u32[]{:S(2)}, u32[]{:S(2)}) collective-permute-start(f32[2,15,128]{2,1,0:T(8,128)S(1)} %get-tuple-element.24), channel_id=1, source_target_pairs={{0,17},{1,16},{2,19},{3,18},{4,21},{5,20},{6,23},{7,22},{8,25},{9,... | collective-permute-start | bytes 46088 | tf_op jit(solution)/shard_map/ppermute | solution.py:238
  15.0 1.8 %collective-permute-done.7 = f32[2,15,128]{2,1,0:T(8,128)S(1)} collective-permute-done((f32[2,15,128]{2,1,0:T(8,128)S(1)}, f32[2,15,128]{2,1,0:T(8,128)S(1)}, u32[]{:S(2)}, u32[]{:S(2)}) %collective-permute-start.7) | collective-permute-done | bytes 15392 | tf_op jit(solution)/shard_map/ppermute | solution.py:238
  16.8 0.2 collective-permute-start.8
  17.0 0.4 %collective-permute-start.6 = (f32[180,128]{1,0:T(8,128)S(1)}, f32[180,128]{1,0:T(8,128)S(1)}, u32[]{:S(2)}, u32[]{:S(2)}) collective-permute-start(f32[180,128]{1,0:T(8,128)S(1)} %get-tuple-element.23.result_ref.own_ref), channel_id=1, source_target_pairs={{0,1},{1,0},{2,3},{3,2},{4,5},{5,4},{6,7},{7,6},{8,9},{9,8},{10,11... | collective-permute-start | bytes 276488 | tf_op jit(solution)/shard_map/ppermute | solution.py:231
  17.4 2.6 %collective-permute-done.8 = f32[2,15,128]{2,1,0:T(8,128)S(1)} collective-permute-done((f32[2,15,128]{2,1,0:T(8,128)S(1)}, f32[2,15,128]{2,1,0:T(8,128)S(1)}, u32[]{:S(2)}, u32[]{:S(2)}) %collective-permute-start.8) | collective-permute-done | bytes 15392 | tf_op jit(solution)/shard_map/ppermute | solution.py:238
  20.0 1.3 %conditional.1 = (f32[2,15,128]{2,1,0:T(8,128)S(1)}) conditional(s32[]{:T(128)} %convert_element_type.3, f32[2,15,128]{2,1,0:T(8,128)S(1)} %pad_maximum_fusion.3, f32[2,15,128]{2,1,0:T(8,128)S(1)} %pad_maximum_fusion.3), branch_computations={%region_0.0_spmd, %region_1.0_spmd} | conditional | bytes 92208 | solution.py:241
  20.1 0.1 collective-permute-start
  20.2 1.1 %collective-permute-done = f32[2,15,128]{2,1,0:T(8,128)S(1)} collective-permute-done((f32[2,15,128]{2,1,0:T(8,128)S(1)}, f32[2,15,128]{2,1,0:T(8,128)S(1)}, u32[]{:S(2)}, u32[]{:S(2)}) %collective-permute-start) | collective-permute-done | bytes 15392 | tf_op jit(solution)/shard_map/cond/branch_1_fun/ppermute | solution.py:241
  21.3 0.0 collective-permute-done.6.passed_ref
  21.3 0.7 %shard_map.89 = (f32[10,1920]{1,0:T(8,128)}, f32[15,128]{1,0:T(8,128)}, f32[15,128]{1,0:T(8,128)}, f32[15,128]{1,0:T(8,128)}, s32[15,128]{1,0:T(8,128)}) custom-call(f32[180,128]{1,0:T(8,128)S(1)} %get-tuple-element.23.result_ref.own_ref, f32[180,128]{1,0:T(8,128)S(1)} %collective-permute-done.6.passed_ref, f32[2,15,128]{2,1,0:T(8,128)S(1)} %get-tuple-element.38.moment_ref, ...), custom_call_target="tpu_custom_call" | custom-call | tf_op jit(solution)/shard_map/pallas_call | solution.py:243
  (10 shorter events, 0.1 us)
Async XLA Ops:
  1.7 5.2 %collective-permute-start.1 = (f32[3,48,128]{2,1,0:T(8,128)S(1)}, f32[3,48,128]{2,1,0:T(8,128)S(1)}, u32[]{:S(2)}, u32[]{:S(2)}) collective-permute-start(f32[3,48,128]{2,1,0:T(8,128)S(1)} %get-tuple-element.21), channel_id=1, source_target_pairs={{0,1},{1,0},{2,3},{3,2},{4,5},{5,4},{6,7},{7,6},{8,9},{9,8},{10,11... | collective-permute-start | bytes 221192 | tf_op jit(solution)/shard_map/ppermute | solution.py:218
  2.4 4.4 %collective-permute-start.4 = (f32[2,48,128]{2,1,0:T(8,128)S(1)}, f32[2,48,128]{2,1,0:T(8,128)S(1)}, u32[]{:S(2)}, u32[]{:S(2)}) collective-permute-start(f32[2,48,128]{2,1,0:T(8,128)S(1)} %get-tuple-element.22), channel_id=1, source_target_pairs={{0,7},{1,6},{2,5},{3,4},{4,3},{5,2},{6,1},{7,0},{8,15},{9,14},{10,... | collective-permute-start | bytes 147464 | tf_op jit(solution)/shard_map/ppermute | solution.py:223
  6.8 3.5 %collective-permute-start.5 = (f32[2,48,128]{2,1,0:T(8,128)S(1)}, f32[2,48,128]{2,1,0:T(8,128)S(1)}, u32[]{:S(2)}, u32[]{:S(2)}) collective-permute-start(f32[2,48,128]{2,1,0:T(8,128)S(1)} %collective-permute-done.4.refs_0_), channel_id=1, source_target_pairs={{0,1},{1,0},{2,3},{3,2},{4,5},{5,4},{6,7},{7,6},{8,9},{9,8},{10,11... | collective-permute-start | bytes 147464 | tf_op jit(solution)/shard_map/ppermute | solution.py:225
  6.9 3.9 %collective-permute-start.3 = (f32[2,48,128]{2,1,0:T(8,128)S(1)}, f32[2,48,128]{2,1,0:T(8,128)S(1)}, u32[]{:S(2)}, u32[]{:S(2)}) collective-permute-start(f32[2,48,128]{2,1,0:T(8,128)S(1)} %pad_maximum_fusion.1), channel_id=1, source_target_pairs={{0,3},{1,2},{2,1},{3,0},{4,7},{5,6},{6,5},{7,4},{8,11},{9,10},{10,... | collective-permute-start | bytes 147464 | tf_op jit(solution)/shard_map/ppermute | solution.py:223
  8.5 3.5 %collective-permute-start.2 = (f32[2,48,128]{2,1,0:T(8,128)S(1)}, f32[2,48,128]{2,1,0:T(8,128)S(1)}, u32[]{:S(2)}, u32[]{:S(2)}) collective-permute-start(f32[2,48,128]{2,1,0:T(8,128)S(1)} %pad_maximum_fusion), channel_id=1, source_target_pairs={{0,5},{1,4},{2,7},{3,6},{4,1},{5,0},{6,3},{7,2},{8,13},{9,12},{10,... | collective-permute-start | bytes 147464 | tf_op jit(solution)/shard_map/ppermute | solution.py:223
  12.6 4.1 %collective-permute-start.7 = (f32[2,15,128]{2,1,0:T(8,128)S(1)}, f32[2,15,128]{2,1,0:T(8,128)S(1)}, u32[]{:S(2)}, u32[]{:S(2)}) collective-permute-start(f32[2,15,128]{2,1,0:T(8,128)S(1)} %get-tuple-element.24), channel_id=1, source_target_pairs={{0,17},{1,16},{2,19},{3,18},{4,21},{5,20},{6,23},{7,22},{8,25},{9,... | collective-permute-start | bytes 46088 | tf_op jit(solution)/shard_map/ppermute | solution.py:238
  16.8 3.2 %collective-permute-start.8 = (f32[2,15,128]{2,1,0:T(8,128)S(1)}, f32[2,15,128]{2,1,0:T(8,128)S(1)}, u32[]{:S(2)}, u32[]{:S(2)}) collective-permute-start(f32[2,15,128]{2,1,0:T(8,128)S(1)} %pad_maximum_fusion.2), channel_id=1, source_target_pairs={{0,9},{1,8},{2,11},{3,10},{4,13},{5,12},{6,15},{7,14},{8,1},{9,0},... | collective-permute-start | bytes 46088 | tf_op jit(solution)/shard_map/ppermute | solution.py:238
  17.0 4.3 %collective-permute-start.6 = (f32[180,128]{1,0:T(8,128)S(1)}, f32[180,128]{1,0:T(8,128)S(1)}, u32[]{:S(2)}, u32[]{:S(2)}) collective-permute-start(f32[180,128]{1,0:T(8,128)S(1)} %get-tuple-element.23.result_ref.own_ref), channel_id=1, source_target_pairs={{0,1},{1,0},{2,3},{3,2},{4,5},{5,4},{6,7},{7,6},{8,9},{9,8},{10,11... | collective-permute-start | bytes 276488 | tf_op jit(solution)/shard_map/ppermute | solution.py:231
  20.1 1.2 %collective-permute-start = (f32[2,15,128]{2,1,0:T(8,128)S(1)}, f32[2,15,128]{2,1,0:T(8,128)S(1)}, u32[]{:S(2)}, u32[]{:S(2)}) collective-permute-start(f32[2,15,128]{2,1,0:T(8,128)S(1)} %param.1), channel_id=1, source_target_pairs={{0,1},{1,0},{2,3},{3,2},{4,5},{5,4},{6,7},{7,6},{8,9},{9,8},{10,11... | collective-permute-start | bytes 46088 | tf_op jit(solution)/shard_map/cond/branch_1_fun/ppermute | solution.py:241
